TPU v7x, 128 devices: a whole 4x4x4 slice. The times are simulated.
128 devices in a mesh: row: 8 (over x_hi, z), col: 16 (over x_lo, y, core).
Axes of the slice: x: 4 (x_hi: 2, x_lo: 2; x = x_hi * 2 + x_lo), y: 4, z: 4, core: 2. Of those that a mesh axis runs over, the one named last changes fastest.
Arguments:
- customer_inputs: bfloat16 [131072, 1024], P(('row', 'col')), may hold values from -6 to 6
- candidate_inputs: bfloat16 [131072, 1024], P(('row', 'col')), may hold values from -6 to 6
- affinity_sharpness: bfloat16 [131072], P(('row', 'col')), may hold values from 4 to 40
- correct_candidate_index: int32 [131072], P(('row', 'col')), may hold values from 0 to 8191
- customer_initial_weights: bfloat16 [1024, 512], replicated, may hold values from -0.1875 to 0.1875
- customer_final_weights: bfloat16 [512, 256], replicated, may hold values from -0.25 to 0.25
- candidate_initial_weights: bfloat16 [1024, 512], replicated, may hold values from -0.1875 to 0.1875
- candidate_final_weights: bfloat16 [512, 256], replicated, may hold values from -0.25 to 0.25
Outputs:
- loss: float32 [], replicated
- grad_user_first: float32 [1024, 512], replicated
- grad_user_second: float32 [512, 256], replicated
- grad_item_first: float32 [1024, 512], replicated
- grad_item_second: float32 [512, 256], replicated
Inputs may be any that keep to these rules, and one draw needn't show every extreme that they name: correct_candidate_index[u] indexes the items of u's group in the order of the steps.
All inputs are finite; a program needn't handle non-finite values.
Results may differ from a plain program's by a relative error of at most 0.015.
Values may be sent and summed in bfloat16 or wider, within the bound.
No kernel may reach another device: no remote copies, remote signals or barrier semaphores. Data moves between devices by JAX's collectives and lax.ppermute only.
A program may use at most 128 MiB of HBM per device.

v0:
```python
import functools
import math
from typing import NamedTuple

import jax
import jax.numpy as jnp
from jax import lax
from jax.experimental import pallas as pl
from jax.experimental.pallas import tpu as pltpu
from jax.sharding import Mesh
from jax.sharding import PartitionSpec as P


EPS = 1e-06
BF = jnp.bfloat16
F32 = jnp.float32
NZ = 4
LANES = 128
ROWS = 256
HOPS = (0, 1, NZ - 1, 2)


def dot(a, b, dims=(1, 0)):
    return lax.dot_general(
        a, b, (((dims[0],), (dims[1],)), ((), ())), preferred_element_type=F32
    )


def cost(flops, nbytes, exps=0):
    return pl.CostEstimate(flops=flops, bytes_accessed=nbytes, transcendentals=exps)


def grant(mib):
    return pltpu.CompilerParams(vmem_limit_bytes=mib * 2**20)


def whole(shape):
    return pl.BlockSpec(shape, lambda *_: (0,) * len(shape))


def in_vmem(n):
    return [pl.BlockSpec(memory_space=pltpu.VMEM)] * n


def forward_kernel(feats, first, second, vec, hidden, out):
    pre = dot(feats[...], first[...])
    h = jnp.maximum(pre, 0.0).astype(BF)
    hidden[...] = h
    o = dot(h, second[...])
    out[...] = o
    inv = lax.rsqrt(jnp.mean(o * o, axis=-1, keepdims=True) + EPS)
    vec[...] = (o * inv).astype(BF)


def tower_forward(feats, first, second):
    m, f = feats.shape
    hid, emb = second.shape
    return pl.pallas_call(
        forward_kernel,
        grid=(m // ROWS,),
        in_specs=[
            pl.BlockSpec((ROWS, f), lambda i: (i, 0)),
            whole(first.shape),
            whole(second.shape),
        ],
        out_specs=[
            pl.BlockSpec((ROWS, emb), lambda i: (i, 0)),
            pl.BlockSpec((ROWS, hid), lambda i: (i, 0)),
            pl.BlockSpec((ROWS, emb), lambda i: (i, 0)),
        ],
        out_shape=[
            jax.ShapeDtypeStruct((m, emb), BF),
            jax.ShapeDtypeStruct((m, hid), BF),
            jax.ShapeDtypeStruct((m, emb), F32),
        ],
        cost_estimate=cost(2 * m * hid * (f + emb), 2 * m * f + 2 * f * hid + 6 * m * emb),
        compiler_params=grant(10),
        name="tower_forward",
    )(feats, first, second)


def first_forward_kernel(feats, first, second, sharp, chosen, vec, hidden, out, meta, x, w1, w2, sems):
    m, f = feats.shape
    steps = m // ROWS
    slices = [pl.ds(k * ROWS, ROWS) for k in range(steps)]
    halves = [pl.ds(k * (f // 2), f // 2) for k in range(2)]
    copies = [
        pltpu.make_async_copy(feats.at[slices[0]], x.at[slices[0]], sems.at[0]),
        pltpu.make_async_copy(first.at[halves[0]], w1.at[halves[0]], sems.at[1]),
        pltpu.make_async_copy(first.at[halves[1]], w1.at[halves[1]], sems.at[2]),
        pltpu.make_async_copy(second, w2, sems.at[3]),
    ]
    copies += [
        pltpu.make_async_copy(feats.at[slices[k]], x.at[slices[k]], sems.at[3 + k])
        for k in range(1, steps)
    ]
    for copy in copies:
        copy.start()
    for which, rows in enumerate((sharp[...].astype(F32), chosen[...].astype(F32))):
        for k in range(rows.shape[0]):
            meta[which : which + 1, k * LANES : (k + 1) * LANES] = rows[k : k + 1, :]
    for copy in copies[:4]:
        copy.wait()
    for k in range(steps):
        if k:
            copies[3 + k].wait()
        here = slice(k * ROWS, (k + 1) * ROWS)
        h = jnp.maximum(dot(x[here, :], w1[...]), 0.0).astype(BF)
        hidden[here, :] = h
        o = dot(h, w2[...])
        out[here, :] = o
        inv = lax.rsqrt(jnp.mean(o * o, axis=-1, keepdims=True) + EPS)
        vec[here, :] = (o * inv).astype(BF)


def first_tower_forward(feats, first, second, sharp, chosen):
    m, f = feats.shape
    hid, emb = second.shape
    return pl.pallas_call(
        first_forward_kernel,
        in_specs=[pl.BlockSpec(memory_space=pltpu.HBM)] * 3 + in_vmem(2),
        out_specs=in_vmem(4),
        out_shape=[
            jax.ShapeDtypeStruct((m, emb), BF),
            jax.ShapeDtypeStruct((m, hid), BF),
            jax.ShapeDtypeStruct((m, emb), F32),
            jax.ShapeDtypeStruct((2, m), F32),
        ],
        scratch_shapes=[
            pltpu.VMEM((m, f), BF),
            pltpu.VMEM((f, hid), BF),
            pltpu.VMEM((hid, emb), BF),
            pltpu.SemaphoreType.DMA((3 + m // ROWS,)),
        ],
        cost_estimate=cost(2 * m * hid * (f + emb), 2 * m * f + 2 * f * hid + 6 * m * emb),
        compiler_params=grant(58),
        name="tower_forward",
    )(feats, first, second, sharp.reshape(-1, LANES), chosen.reshape(-1, LANES))


def first_item(slot, rows):
    row = lax.axis_index("row")
    z = lax.rem(row, NZ)
    return (row - z + lax.rem(z + (NZ - HOPS[slot]), NZ)) * rows


def scores_kernel(blocks, n_items, n_users, n_sums, last, *refs):
    items, refs = refs[:n_items], refs[n_items:]
    users, metas, refs = refs[:n_users], refs[n_users : 2 * n_users], refs[2 * n_users :]
    before, refs = refs[:n_sums], refs[n_sums:]
    exps, after = refs[: len(blocks)], refs[len(blocks) :]
    for side in range(n_users):
        n, emb = users[side].shape
        u = users[side][...]
        scale = metas[side][0:1, :] * (math.log2(math.e) / emb)
        total = jnp.zeros((8, n), F32)
        picked = jnp.zeros((8, n), F32)
        for block, (at, slot, whose) in enumerate(blocks):
            if whose != side:
                continue
            m = items[at].shape[0]
            target = metas[side][1:2, :].astype(jnp.int32) - first_item(slot, m)
            for r in range(0, m, ROWS):
                logits = dot(items[at][r : r + ROWS, :], u, (1, 1)) * scale
                e = jnp.exp2(logits)
                exps[block][r : r + ROWS, :] = e.astype(BF)
                total = total + jnp.sum(e.reshape(ROWS // 8, 8, n), axis=0)
                rows = lax.broadcasted_iota(jnp.int32, (ROWS, n), 0)
                hit = jnp.where(rows == target - r, logits, 0.0)
                picked = picked + jnp.sum(hit.reshape(ROWS // 8, 8, n), axis=0)
        total = jnp.sum(total, axis=0, keepdims=True)
        picked = jnp.sum(picked, axis=0, keepdims=True)
        if n_sums:
            total = total + before[side][0:1, :]
            picked = picked + before[side][1:2, :]
        if last:
            after[0][side : side + 1, :] = total
            after[0][2 + side : 3 + side, :] = picked
        else:
            after[side][0:1, :] = total
            after[side][1:2, :] = picked


def scores(blocks, items, users, metas, sums, last=False):
    n, emb = users[0].shape
    m = items[0].shape[0]
    results = [jax.ShapeDtypeStruct((m, n), BF)] * len(blocks)
    if last:
        results += [jax.ShapeDtypeStruct((4, n), F32)]
    else:
        results += [jax.ShapeDtypeStruct((2, n), F32)] * len(users)
    operands = (*items, *users, *metas, *sums)
    count = len(blocks)
    out = pl.pallas_call(
        functools.partial(scores_kernel, blocks, len(items), len(users), len(sums), last),
        in_specs=in_vmem(len(operands)),
        out_specs=in_vmem(len(results)),
        out_shape=results,
        cost_estimate=cost(2 * count * m * n * emb, count * 2 * m * n, count * m * n),
        compiler_params=grant(10),
        name="scores",
    )(*operands)
    return out[:count], out[count:]


def three_terms(value):
    hi = value.astype(BF).astype(F32)
    mid = (value - hi).astype(BF).astype(F32)
    low = value - hi - mid
    lane = lax.broadcasted_iota(jnp.int32, (8, LANES), 1)
    return jnp.where(lane == 0, hi, jnp.where(lane == 1, mid, jnp.where(lane == 2, low, 0.0)))


class Plan(NamedTuple):
    blocks: tuple
    send: tuple = ()
    keep: tuple = ()
    had: tuple = ()
    users_in: tuple = ()
    users_out: tuple = ()
    users_send: tuple = ()
    loss: bool = False

    def slots(self):
        return tuple(sorted({slot for slot, _ in self.blocks}))

    def sides(self):
        return tuple(sorted({side for _, side in self.blocks}))


def vectors_kernel(plan, unit, *refs):
    refs = iter(refs)
    mine, theirs = next(refs), next(refs)
    items = {slot: next(refs) for slot in plan.slots()}
    users = {side: next(refs) for side in plan.sides()}
    metas = {side: next(refs) for side in plan.sides()}
    exps = {block: next(refs) for block in plan.blocks}
    grad_items = {slot: next(refs) for slot in plan.had}
    grad_users = {side: next(refs) for side in plan.users_in}
    items_out = {slot: next(refs) for slot in plan.send + plan.keep}
    users_out = {side: next(refs) for side in plan.users_out + plan.users_send}
    if plan.loss:
        loss = next(refs)
    item_acc, user_acc = next(refs), next(refs)
    slots_done, sides_done = set(), set()
    for place, (slot, side) in enumerate(plan.blocks):
        v = items[slot][...]
        m, n = v.shape[0], users[side].shape[0]
        mass = mine[side : side + 1, :] + theirs[1 - side : 2 - side, :]
        sharp = metas[side][0:1, :] * unit
        weight = sharp / mass
        target = metas[side][1:2, :].astype(jnp.int32) - first_item(slot, m)
        if plan.loss and side == 0:
            local = jnp.sum(jnp.log(mass), axis=1, keepdims=True)
            picked = jnp.sum(mine[2:3, :] + mine[3:4, :], axis=1, keepdims=True)
            loss[...] = jnp.broadcast_to(local - math.log(2.0) * picked, loss.shape)
        later = plan.blocks[place + 1 :]
        slot_ends = slot not in [x for x, _ in later]
        side_ends = side not in [x for _, x in later]
        for r in range(0, n, ROWS):
            cols = slice(r, r + ROWS)
            e = exps[slot, side][:, cols].astype(F32) * weight[:, cols]
            rows = lax.broadcasted_iota(jnp.int32, e.shape, 0)
            d = jnp.where(rows == target[:, cols], e - sharp[:, cols], e).astype(BF)
            grad = dot(d, users[side][cols, :])
            if slot in slots_done or r:
                grad = grad + item_acc[...]
            elif slot in grad_items:
                grad = grad + grad_items[slot][...]
            if slot_ends and r + ROWS == n:
                items_out[slot][...] = grad.astype(items_out[slot].dtype)
            else:
                item_acc[...] = grad
            grad = dot(v, d, (0, 0))
            if side in sides_done:
                grad = grad + user_acc[side, :, cols]
            elif side in grad_users:
                grad = grad + grad_users[side][:, cols]
            if side_ends:
                users_out[side][:, cols] = grad.astype(users_out[side].dtype)
            else:
                user_acc[side, :, cols] = grad
        slots_done.add(slot)
        sides_done.add(side)


def vector_grads(plan, unit, mine, theirs, items, users, metas, exps, grad_items, grad_users):
    n, emb = users[0].shape
    m = items[0].shape[0]
    operands = [mine, theirs]
    operands += [items[slot] for slot in plan.slots()]
    operands += [users[side] for side in plan.sides()]
    operands += [metas[side] for side in plan.sides()]
    operands += [exps[side][slot] for slot, side in plan.blocks]
    operands += [grad_items[slot] for slot in plan.had]
    operands += [grad_users[side] for side in plan.users_in]
    results = [jax.ShapeDtypeStruct((m, emb), BF) for _ in plan.send]
    results += [jax.ShapeDtypeStruct((m, emb), F32) for _ in plan.keep]
    results += [jax.ShapeDtypeStruct((emb, n), F32) for _ in plan.users_out]
    results += [jax.ShapeDtypeStruct((emb, n), BF) for _ in plan.users_send]
    if plan.loss:
        results += [jax.ShapeDtypeStruct((8, LANES), F32)]
    count = len(plan.blocks)
    out = pl.pallas_call(
        functools.partial(vectors_kernel, plan, unit),
        in_specs=in_vmem(len(operands)),
        out_specs=in_vmem(len(results)),
        out_shape=results,
        scratch_shapes=[pltpu.VMEM((m, emb), F32), pltpu.VMEM((2, emb, n), F32)],
        cost_estimate=cost(4 * count * m * n * emb, 2 * count * m * n + 10 * n * emb),
        compiler_params=grant(10),
        name="vector_grads",
    )(*operands)
    out = iter(out)
    for slot in plan.send + plan.keep:
        grad_items[slot] = next(out)
    for side in plan.users_out + plan.users_send:
        grad_users[side] = next(out)
    return next(out, None)


def backward_kernel(turned, n_other, has_loss, *refs):
    feats, second, hidden, out, own = refs[:5]
    others = refs[5 : 5 + n_other]
    refs = refs[5 + n_other :]
    if has_loss:
        loss, refs = refs[0], refs[1:]
    kept, sent, grad_out, grad_pre, first, last = refs
    m, f = feats.shape
    hid, _ = second.shape
    for r in range(0, m, ROWS):
        here = slice(r, r + ROWS)
        at = (slice(None), here) if turned else (here, slice(None))
        grad = own[at].astype(F32)
        for other in others:
            grad = grad + other[at].astype(F32)
        if turned:
            grad = grad.T
        grad = grad.astype(BF).astype(F32)
        o = out[here, :]
        inv = lax.rsqrt(jnp.mean(o * o, axis=-1, keepdims=True) + EPS)
        normed = o * inv
        g = inv * (grad - normed * jnp.mean(grad * normed, axis=-1, keepdims=True))
        g = g.astype(BF)
        grad_out[here, :] = g
        back = dot(g, second[...], (1, 1))
        grad_pre[here, :] = jnp.where(hidden[here, :] > 0, back, 0.0).astype(BF)
    for r in range(0, hid, ROWS):
        here = slice(r, r + ROWS)
        last[here, :] = dot(hidden[:, here], grad_out[...], (0, 0)).astype(BF)
    for r in range(0, f, ROWS):
        here = slice(r, r + ROWS)
        first[here, :] = dot(feats[:, here], grad_pre[...], (0, 0)).astype(BF)
    core = lax.axis_index("core")
    half = kept.shape[0]
    for which in range(2):

        @pl.when(core == which)
        def _():
            targets = (sent, kept) if which else (kept, sent)
            for array, k, start, rows, place, at in pieces(first, last, half):
                targets[place][at : at + rows, :] = array[
                    start : start + rows, k * LANES : (k + 1) * LANES
                ]

    if has_loss:
        sent[half : half + 8, :] = three_terms(loss[...]).astype(BF)


def pieces(first, second, half):
    at = 0
    for array in (first, second):
        rows, cols = array.shape
        for k in range(cols // LANES):
            done = 0
            while done < rows:
                place, inside = divmod(at, half)
                take = min(rows - done, half - inside)
                yield array, k, done, take, place, inside
                done += take
                at += take


def tower_backward(feats, second, hidden, out, own, others, turned, loss=None):
    m, f = feats.shape
    hid, emb = second.shape
    half = (f * hid + hid * emb) // LANES // 2
    extra = () if loss is None else (loss,)
    operands = (feats, second, hidden, out, own, *others, *extra)
    shapes = [(half, LANES), (half + 8 * len(extra), LANES)]
    return pl.pallas_call(
        functools.partial(backward_kernel, turned, len(others), len(extra)),
        in_specs=in_vmem(len(operands)),
        out_specs=in_vmem(2),
        out_shape=[jax.ShapeDtypeStruct(shape, BF) for shape in shapes],
        scratch_shapes=[
            pltpu.VMEM((m, emb), BF),
            pltpu.VMEM((m, hid), BF),
            pltpu.VMEM((f, hid), BF),
            pltpu.VMEM((hid, emb), BF),
        ],
        cost_estimate=cost(2 * m * hid * (f + 2 * emb), 2 * m * f + 4 * f * hid + 10 * m * emb),
        compiler_params=grant(12),
        name="tower_backward",
    )(*operands)


def pair_kernel(n_peers, share, kept_users, got_users, kept_items, got_items, loss, out):
    half = n_peers * share
    for k, (kept, got) in enumerate(((kept_users, got_users), (kept_items, got_items))):
        pair = kept[...].astype(F32) + got[0:half, :].astype(F32)
        out[:, k * share : (k + 1) * share, :] = pair.astype(BF).reshape(n_peers, share, LANES)
    other = jnp.sum(got_users[half : half + 8, :].astype(F32), axis=1, keepdims=True)
    total = three_terms(loss[...] + other).astype(BF)
    out[:, 2 * share : 2 * share + 8, :] = jnp.broadcast_to(total[None], (n_peers, 8, LANES))


def share_kernel(count, parts, out, loss):
    n_peers, rows, _ = parts.shape
    total = jnp.zeros((rows, LANES), F32)
    for k in range(n_peers):
        total = total + parts[k].astype(F32)
    loss[0, 0] = jnp.sum(total[rows - 8 : rows - 7, :]) / count
    summed = total[: rows - 8].astype(BF)
    for k in range(n_peers):
        out[k] = summed


def unpack_kernel(mine, theirs, *outs):
    n_peers, rows, _ = mine.shape
    share = rows // 2
    half = n_peers * share
    core = lax.axis_index("core")
    for which in range(2):

        @pl.when(core == which)
        def _():
            halves = (theirs, mine) if which else (mine, theirs)
            for tower in range(2):
                values = [
                    x[:, tower * share : (tower + 1) * share, :].reshape(half, LANES) for x in halves
                ]
                first, second = outs[2 * tower : 2 * tower + 2]
                for out, k, start, count, place, at in pieces(first, second, half):
                    out[start : start + count, k * LANES : (k + 1) * LANES] = values[place][
                        at : at + count, :
                    ].astype(F32)


def sum_over_all(user_parts, item_parts, loss, shapes, other_core, count):
    (kept_users, sent_users), (kept_items, sent_items) = user_parts, item_parts
    peers = ("row", "chip")
    n_peers = lax.axis_size("row") * lax.axis_size("chip")
    share = kept_users.shape[0] // n_peers
    got_users, got_items = other_core(sent_users), other_core(sent_items)
    to_sum = pl.pallas_call(
        functools.partial(pair_kernel, n_peers, share),
        in_specs=in_vmem(5),
        out_specs=in_vmem(1)[0],
        out_shape=jax.ShapeDtypeStruct((n_peers, 2 * share + 8, LANES), BF),
        compiler_params=grant(10),
        name="pair",
    )(kept_users, got_users, kept_items, got_items, loss)
    parts = lax.all_to_all(to_sum, peers, 0, 0, tiled=True)
    to_share, loss = pl.pallas_call(
        functools.partial(share_kernel, count),
        in_specs=in_vmem(1),
        out_specs=[in_vmem(1)[0], pl.BlockSpec(memory_space=pltpu.SMEM)],
        out_shape=[
            jax.ShapeDtypeStruct((n_peers, 2 * share, LANES), BF),
            jax.ShapeDtypeStruct((1, 1), F32),
        ],
        compiler_params=grant(10),
        name="share",
    )(parts)
    mine = lax.all_to_all(to_share, peers, 0, 0, tiled=True)
    theirs = other_core(mine)
    grads = pl.pallas_call(
        unpack_kernel,
        in_specs=in_vmem(2),
        out_specs=in_vmem(4),
        out_shape=[jax.ShapeDtypeStruct(s, F32) for s in shapes],
        compiler_params=grant(14),
        name="unpack",
    )(mine, theirs)
    return (loss.reshape(()), *grads)


def step(
    customer_inputs,
    candidate_inputs,
    affinity_sharpness,
    correct_candidate_index,
    customer_initial_weights,
    customer_final_weights,
    candidate_initial_weights,
    candidate_final_weights,
):
    m, f = customer_inputs.shape
    hid, emb = customer_final_weights.shape
    n_row = lax.axis_size("row")
    n_all = n_row * lax.axis_size("chip") * lax.axis_size("core")

    def along_z(value, hop):
        pairs = [(a * NZ + k, a * NZ + (k + hop) % NZ) for a in range(n_row // NZ) for k in range(NZ)]
        return lax.ppermute(value, "row", pairs)

    def partner(value):
        return lax.ppermute(value, "row", [(k, (k + NZ) % n_row) for k in range(n_row)])

    def other_core(value):
        return lax.ppermute(value, "core", [(0, 1), (1, 0)])

    item_vec, item_hidden, item_out, meta = first_tower_forward(
        candidate_inputs,
        candidate_initial_weights,
        candidate_final_weights,
        affinity_sharpness,
        correct_candidate_index,
    )
    metas = (meta, partner(meta))
    items = [item_vec]
    for slot in range(1, NZ):
        items.append(along_z(item_vec, HOPS[slot]))
    user_vec, user_hidden, user_out = tower_forward(
        customer_inputs, customer_initial_weights, customer_final_weights
    )
    users = (user_vec, partner(user_vec))

    exps = [[None] * NZ, [None] * NZ]
    (exps[0][0],), (own_sums,) = scores(((0, 0, 0),), items[:1], users[:1], metas[:1], ())
    exps[0][1:3], (own_sums,) = scores(
        ((0, 1, 0), (1, 2, 0)), items[1:3], users[:1], metas[:1], (own_sums,)
    )
    exps[1][0:3], (other_sums,) = scores(
        ((0, 0, 0), (1, 1, 0), (2, 2, 0)), items[:3], users[1:], metas[1:], ()
    )
    (exps[0][3], exps[1][3]), (mine,) = scores(
        ((0, 3, 0), (0, 3, 1)), items[3:], users, metas, (own_sums, other_sums), last=True
    )
    theirs = partner(mine)

    unit = 1.0 / (emb * m)
    own, other = 0, 1
    grad_items, grad_users = {}, {}
    arrived = []
    plans = (
        Plan(((3, other), (3, own)), send=(3,), users_out=(other, own)),
        Plan(((1, other), (2, other), (0, other)), keep=(1, 2, 0), users_in=(other,), users_send=(other,)),
        Plan(((1, own),), send=(1,), had=(1,), users_in=(own,), users_out=(own,)),
        Plan(((2, own),), send=(2,), had=(2,), users_in=(own,), users_out=(own,)),
        Plan(((0, own),), keep=(0,), had=(0,), users_in=(own,), users_out=(own,), loss=True),
    )
    for plan in plans:
        loss = vector_grads(
            plan, unit, mine, theirs, items, users, metas, exps, grad_items, grad_users
        )
        for slot in plan.send:
            arrived.append(along_z(grad_items[slot], NZ - HOPS[slot]))
        for side in plan.users_send:
            arrived_users = partner(grad_users[side])
    user_parts = tower_backward(
        customer_inputs,
        customer_final_weights,
        user_hidden,
        user_out,
        grad_users[own],
        [arrived_users],
        True,
        loss,
    )
    item_parts = tower_backward(
        candidate_inputs, candidate_final_weights, item_hidden, item_out, grad_items[0], arrived, False
    )
    return sum_over_all(
        user_parts, item_parts, loss, [(f, hid), (hid, emb)] * 2, other_core, float(m * n_all)
    )


def solution(mesh):
    n_row, n_col = mesh.devices.shape
    fine = Mesh(mesh.devices.reshape(n_row, n_col // 2, 2), ("row", "chip", "core"))
    every = ("row", "chip", "core")
    placed = (P(every, None), P(every, None), P(every), P(every), P(), P(), P(), P())
    return jax.shard_map(
        step, mesh=fine, in_specs=placed, out_specs=(P(), P(), P(), P(), P()), check_vma=False
    )
```

profile of v0, /device:TPU:1, one launch (start us, length us, event | category | flops | bytes accessed | tf_op | source)
XLA Modules:
  0.0 155.2 jit_solution(5654892489410912740)
XLA Ops:
  0.7 6.6 %tower_forward.3 = (bf16[1024,256]{1,0:T(8,128)(2,1)}, bf16[1024,512]{1,0:T(8,128)(2,1)}, f32[1024,256]{1,0:T(8,128)}, f32[2,1024]{1,0:T(2,128)}) custom-call(bf16[1024,1024]{1,0:T(8,128)(2,1)} %refs_0_.3, bf16[1024,512]{1,0:T(8,128)(2,1)} %first.3, bf16[512,256]{1,0:T(8,128)(2,1)} %refs_1_.3, bf16[8,128]{1,0:T(8,128)(2,1)} %bitcast.4, s32[8,128]{1,0:T(8,128)} %bitcast.3), custom_call_target="tpu_custom_call" | custom-call | flops 1342177280 | bytes 4718592 | tf_op jit(solution)/shard_map/tower_forward/pallas_call | solution.py:119
  7.3 4.6 %collective-permute-start.4 = (bf16[1024,256]{1,0:T(8,128)(2,1)}, bf16[1024,256]{1,0:T(8,128)(2,1)S(1)}, u32[]{:S(2)}, u32[]{:S(2)}) collective-permute-start(bf16[1024,256]{1,0:T(8,128)(2,1)} %get-tuple-element.50.refs_0_.refs_2_), channel_id=1, source_target_pairs={{0,48},{16,0},{32,16},{48,32},{64,112},{80,64},{96,80},{112,96},{1... | collective-permute-start | bytes 1572872 | tf_op jit(solution)/shard_map/ppermute | solution.py:506
  11.9 2.9 %tower_forward.2 = (bf16[1024,256]{1,0:T(8,128)(2,1)S(1)}, bf16[1024,512]{1,0:T(8,128)(2,1)S(1)}, f32[1024,256]{1,0:T(8,128)S(1)}) custom-call(bf16[1024,1024]{1,0:T(8,128)(2,1)S(1)} %copy-done.1, bf16[1024,512]{1,0:T(8,128)(2,1)S(1)} %copy-done.8, bf16[512,256]{1,0:T(8,128)(2,1)S(1)} %copy-done.6), custom_call_target="tpu_custom_call" | custom-call | flops 1342177280 | bytes 4718592 | tf_op jit(solution)/shard_map/tower_forward/pallas_call | solution.py:58
  14.8 2.8 %collective-permute-start.1 = (bf16[1024,256]{1,0:T(8,128)(2,1)S(1)}, bf16[1024,256]{1,0:T(8,128)(2,1)S(1)}, u32[]{:S(2)}, u32[]{:S(2)}) collective-permute-start(bf16[1024,256]{1,0:T(8,128)(2,1)S(1)} %get-tuple-element.51.refs_1_.refs_2_.refs_3_), channel_id=1, source_target_pairs={{0,64},{16,80},{32,96},{48,112},{64,0},{80,16},{96,32},{112,48},{1... | collective-permute-start | bytes 1572872 | tf_op jit(solution)/shard_map/ppermute | solution.py:509
  20.5 13.4 %collective-permute-done.4.refs_1_.refs_2_.refs_4_ = bf16[1024,256]{1,0:T(8,128)(2,1)S(1)} collective-permute-done((bf16[1024,256]{1,0:T(8,128)(2,1)}, bf16[1024,256]{1,0:T(8,128)(2,1)S(1)}, u32[]{:S(2)}, u32[]{:S(2)}) %collective-permute-start.4) | collective-permute-done | bytes 524320 | tf_op jit(solution)/shard_map/ppermute | solution.py:506
  33.9 2.5 %scores.5 = (bf16[1024,1024]{1,0:T(8,128)(2,1)S(1)}, bf16[1024,1024]{1,0:T(8,128)(2,1)S(1)}, f32[2,1024]{1,0:T(2,128)S(1)}) custom-call(bf16[1024,256]{1,0:T(8,128)(2,1)S(1)} %collective-permute-done.3.refs_0_.refs_1_.refs_3_.refs_2_, bf16[1024,256]{1,0:T(8,128)(2,1)S(1)} %collective-permute-done.4.refs_1_.refs_2_.refs_4_, ...), custom_call_target="tpu_custom_call" | custom-call | flops 1073741824 | bytes 4194304 | tf_op jit(solution)/shard_map/scores/pallas_call | solution.py:194
  36.5 3.6 %scores.6 = (bf16[1024,1024]{1,0:T(8,128)(2,1)S(1)}, bf16[1024,1024]{1,0:T(8,128)(2,1)S(1)}, bf16[1024,1024]{1,0:T(8,128)(2,1)S(1)}, f32[2,1024]{1,0:T(2,128)S(1)}) custom-call(bf16[1024,256]{1,0:T(8,128)(2,1)S(1)} %copy-done.4, bf16[1024,256]{1,0:T(8,128)(2,1)S(1)} %collective-permute-done.3.refs_0_.refs_1_.refs_3_.refs_2_, ...), custom_call_target="tpu_custom_call" | custom-call | flops 1610612736 | bytes 6291456 | tf_op jit(solution)/shard_map/scores/pallas_call | solution.py:194
  40.0 2.4 %scores.7 = (bf16[1024,1024]{1,0:T(8,128)(2,1)S(1)}, bf16[1024,1024]{1,0:T(8,128)(2,1)S(1)}, f32[4,1024]{1,0:T(4,128)S(1)}) custom-call(bf16[1024,256]{1,0:T(8,128)(2,1)S(1)} %collective-permute-done.refs_0_.refs_2_, bf16[1024,256]{1,0:T(8,128)(2,1)S(1)} %get-tuple-element.51.refs_1_.refs_2_.refs_3_, ...), custom_call_target="tpu_custom_call" | custom-call | flops 1073741824 | bytes 4194304 | tf_op jit(solution)/shard_map/scores/pallas_call | solution.py:194
  42.5 3.0 %collective-permute-start.5 = (f32[4,1024]{1,0:T(4,128)S(1)}, f32[4,1024]{1,0:T(4,128)S(1)}, u32[]{:S(2)}, u32[]{:S(2)}) collective-permute-start(f32[4,1024]{1,0:T(4,128)S(1)} %get-tuple-element.56.refs_0_), channel_id=1, source_target_pairs={{0,64},{16,80},{32,96},{48,112},{64,0},{80,16},{96,32},{112,48},{1... | collective-permute-start | bytes 49160 | tf_op jit(solution)/shard_map/ppermute | solution.py:509
  46.9 2.4 %vector_grads.5 = (bf16[1024,256]{1,0:T(8,128)(2,1)S(1)}, f32[256,1024]{1,0:T(8,128)S(1)}, f32[256,1024]{1,0:T(8,128)S(1)}) custom-call(f32[4,1024]{1,0:T(4,128)S(1)} %get-tuple-element.56.refs_0_, f32[4,1024]{1,0:T(4,128)S(1)} %collective-permute-done.5.refs_1_, bf16[1024,256]{1,0:T(8,128)(2,1)S(1)} %collective-permute-done.refs_0_.refs_2_, ...), custom_call_target="tpu_custom_call" | custom-call | flops 2147483648 | bytes 6815744 | tf_op jit(solution)/shard_map/vector_grads/pallas_call | solution.py:304
  49.3 3.5 %vector_grads.6 = (f32[1024,256]{1,0:T(8,128)S(1)}, f32[1024,256]{1,0:T(8,128)S(1)}, f32[1024,256]{1,0:T(8,128)S(1)}, bf16[256,1024]{1,0:T(8,128)(2,1)S(1)}) custom-call(f32[4,1024]{1,0:T(4,128)S(1)} %get-tuple-element.56.refs_0_, f32[4,1024]{1,0:T(4,128)S(1)} %collective-permute-done.5.refs_1_, bf16[1024,256]{1,0:T(8,128)(2,1)S(1)} %copy-done.4, ...), custom_call_target="tpu_custom_call" | custom-call | flops 3221225472 | bytes 8912896 | tf_op jit(solution)/shard_map/vector_grads/pallas_call | solution.py:304
  52.8 2.8 %collective-permute-start.6 = (bf16[256,1024]{1,0:T(8,128)(2,1)S(1)}, bf16[256,1024]{1,0:T(8,128)(2,1)S(1)}, u32[]{:S(2)}, u32[]{:S(2)}) collective-permute-start(bf16[256,1024]{1,0:T(8,128)(2,1)S(1)} %get-tuple-element.73), channel_id=1, source_target_pairs={{0,64},{16,80},{32,96},{48,112},{64,0},{80,16},{96,32},{112,48},{1... | collective-permute-start | bytes 1572872 | tf_op jit(solution)/shard_map/ppermute | solution.py:509
  58.4 3.5 %collective-permute-start.9 = (bf16[1024,256]{1,0:T(8,128)(2,1)S(1)}, bf16[1024,256]{1,0:T(8,128)(2,1)S(1)}, u32[]{:S(2)}, u32[]{:S(2)}) collective-permute-start(bf16[1024,256]{1,0:T(8,128)(2,1)S(1)} %get-tuple-element.81), channel_id=1, source_target_pairs={{0,48},{16,0},{32,16},{48,32},{64,112},{80,64},{96,80},{112,96},{1... | collective-permute-start | bytes 1572872 | tf_op jit(solution)/shard_map/ppermute | solution.py:506
  64.5 3.1 %tower_backward.2 = (bf16[2560,128]{1,0:T(8,128)(2,1)S(1)}, bf16[2568,128]{1,0:T(8,128)(2,1)S(1)}) custom-call(bf16[1024,1024]{1,0:T(8,128)(2,1)S(1)} %copy-done.1, bf16[512,256]{1,0:T(8,128)(2,1)S(1)} %copy-done.6, bf16[1024,512]{1,0:T(8,128)(2,1)S(1)} %get-tuple-element.48.refs_2_, f32[1024,256]{1,0:T(8,128)S(1)} %get-tuple-element.49.refs_3_, ...), custom_call_target="tpu_custom_call" | custom-call | flops 1610612736 | bytes 6815744 | tf_op jit(solution)/shard_map/tower_backward/pallas_call | solution.py:391
  67.5 5.3 %collective-permute-start.7 = (bf16[2568,128]{1,0:T(8,128)(2,1)S(1)}, bf16[2568,128]{1,0:T(8,128)(2,1)S(1)}, u32[]{:S(2)}, u32[]{:S(2)}) collective-permute-start(bf16[2568,128]{1,0:T(8,128)(2,1)S(1)} %get-tuple-element.76), channel_id=1, source_target_pairs={{0,1},{1,0},{2,3},{3,2},{4,5},{5,4},{6,7},{7,6},{8,9},{9,8},{10,11... | collective-permute-start | bytes 1972232 | tf_op jit(solution)/shard_map/ppermute | solution.py:512
  73.8 9.6 %collective-permute-done.8.refs_5_ = bf16[1024,256]{1,0:T(8,128)(2,1)S(1)} collective-permute-done((bf16[1024,256]{1,0:T(8,128)(2,1)S(1)}, bf16[1024,256]{1,0:T(8,128)(2,1)S(1)}, u32[]{:S(2)}, u32[]{:S(2)}) %collective-permute-start.8) | collective-permute-done | bytes 524320 | tf_op jit(solution)/shard_map/ppermute | solution.py:506
  83.4 2.8 %tower_backward.3 = (bf16[2560,128]{1,0:T(8,128)(2,1)S(1)}, bf16[2560,128]{1,0:T(8,128)(2,1)S(1)}) custom-call(bf16[1024,1024]{1,0:T(8,128)(2,1)S(1)} %copy-done, bf16[512,256]{1,0:T(8,128)(2,1)S(1)} %copy-done.5, bf16[1024,512]{1,0:T(8,128)(2,1)S(1)} %copy-done.2, f32[1024,256]{1,0:T(8,128)S(1)} %copy-done.3, f32[1024,256]{1,0:T(8,128)S(1)} %get-tuple-element.79.refs_4_, ...), custom_call_target="tpu_custom_call" | custom-call | flops 1610612736 | bytes 6815744 | tf_op jit(solution)/shard_map/tower_backward/pallas_call | solution.py:391
  86.2 3.9 %collective-permute-start.11 = (bf16[2560,128]{1,0:T(8,128)(2,1)S(1)}, bf16[2560,128]{1,0:T(8,128)(2,1)S(1)}, u32[]{:S(2)}, u32[]{:S(2)}) collective-permute-start(bf16[2560,128]{1,0:T(8,128)(2,1)S(1)} %get-tuple-element.84), channel_id=1, source_target_pairs={{0,1},{1,0},{2,3},{3,2},{4,5},{5,4},{6,7},{7,6},{8,9},{9,8},{10,11... | collective-permute-start | bytes 1966088 | tf_op jit(solution)/shard_map/ppermute | solution.py:512
  90.1 1.7 %collective-permute-done.11.got_items = bf16[2560,128]{1,0:T(8,128)(2,1)S(1)} collective-permute-done((bf16[2560,128]{1,0:T(8,128)(2,1)S(1)}, bf16[2560,128]{1,0:T(8,128)(2,1)S(1)}, u32[]{:S(2)}, u32[]{:S(2)}) %collective-permute-start.11) | collective-permute-done | bytes 655392 | tf_op jit(solution)/shard_map/ppermute | solution.py:512
  92.6 28.8 %all_to_all.10.parts = bf16[64,88,128]{2,1,0:T(8,128)(2,1)S(1)} all-to-all(bf16[64,88,128]{2,1,0:T(8,128)(2,1)S(1)} %pair.1), channel_id=1, replica_groups=mesh['row'=8,'chip'=8,'core'=2] {'row','chip'}, dimensions={0} | all-to-all | bytes 2883584 | tf_op jit(solution)/shard_map/all_to_all | solution.py:464
  122.2 24.8 %all_to_all.11.mine = bf16[64,80,128]{2,1,0:T(8,128)(2,1)S(1)} all-to-all(bf16[64,80,128]{2,1,0:T(8,128)(2,1)S(1)} %get-tuple-element.86), channel_id=1, replica_groups=mesh['row'=8,'chip'=8,'core'=2] {'row','chip'}, dimensions={0} | all-to-all | bytes 2621440 | tf_op jit(solution)/shard_map/all_to_all | solution.py:476
  147.0 2.5 %collective-permute-start.12 = (bf16[64,80,128]{2,1,0:T(8,128)(2,1)S(1)}, bf16[64,80,128]{2,1,0:T(8,128)(2,1)S(1)}, u32[]{:S(2)}, u32[]{:S(2)}) collective-permute-start(bf16[64,80,128]{2,1,0:T(8,128)(2,1)S(1)} %all_to_all.11.mine), channel_id=1, source_target_pairs={{0,1},{1,0},{2,3},{3,2},{4,5},{5,4},{6,7},{7,6},{8,9},{9,8},{10,11... | collective-permute-start | bytes 3932168 | tf_op jit(solution)/shard_map/ppermute | solution.py:512
  149.5 2.7 %collective-permute-done.12.theirs = bf16[64,80,128]{2,1,0:T(8,128)(2,1)S(1)} collective-permute-done((bf16[64,80,128]{2,1,0:T(8,128)(2,1)S(1)}, bf16[64,80,128]{2,1,0:T(8,128)(2,1)S(1)}, u32[]{:S(2)}, u32[]{:S(2)}) %collective-permute-start.12) | collective-permute-done | bytes 1310752 | tf_op jit(solution)/shard_map/ppermute | solution.py:512
  152.2 3.0 %unpack.1 = (f32[1024,512]{1,0:T(8,128)}, f32[512,256]{1,0:T(8,128)}, f32[1024,512]{1,0:T(8,128)}, f32[512,256]{1,0:T(8,128)}) custom-call(bf16[64,80,128]{2,1,0:T(8,128)(2,1)S(1)} %all_to_all.11.mine, bf16[64,80,128]{2,1,0:T(8,128)(2,1)S(1)} %collective-permute-done.12.theirs), custom_call_target="tpu_custom_call" | custom-call | tf_op jit(solution)/shard_map/unpack/pallas_call | solution.py:478
  (38 shorter events, 11.9 us)
Async XLA Ops:
  0.6 11.3 %copy-start.1 = (bf16[1024,1024]{1,0:T(8,128)(2,1)S(1)}, bf16[1024,1024]{1,0:T(8,128)(2,1)}, u32[]{:S(2)}) copy-start(bf16[1024,1024]{1,0:T(8,128)(2,1)} %refs_0_.2) | copy-start | bytes 6291460
  0.6 11.3 %copy-start.6 = (bf16[512,256]{1,0:T(8,128)(2,1)S(1)}, bf16[512,256]{1,0:T(8,128)(2,1)}, u32[]{:S(2)}) copy-start(bf16[512,256]{1,0:T(8,128)(2,1)} %refs_1_.2) | copy-start | bytes 786436
  0.7 11.3 %copy-start.8 = (bf16[1024,512]{1,0:T(8,128)(2,1)S(1)}, bf16[1024,512]{1,0:T(8,128)(2,1)}, u32[]{:S(2)}) copy-start(bf16[1024,512]{1,0:T(8,128)(2,1)} %first.2) | copy-start | bytes 3145732
  7.2 10.4 %copy-start.4 = (bf16[1024,256]{1,0:T(8,128)(2,1)S(1)}, bf16[1024,256]{1,0:T(8,128)(2,1)}, u32[]{:S(2)}) copy-start(bf16[1024,256]{1,0:T(8,128)(2,1)} %get-tuple-element.50.refs_0_.refs_2_) | copy-start | bytes 1572868
  7.3 11.7 %copy-start.7 = (f32[2,1024]{1,0:T(2,128)S(1)}, f32[2,1024]{1,0:T(2,128)}, u32[]{:S(2)}) copy-start(f32[2,1024]{1,0:T(2,128)} %get-tuple-element.52.refs_2_.refs_3_.refs_5_.refs_4_) | copy-start | bytes 24580
  7.3 26.7 %collective-permute-start.4 = (bf16[1024,256]{1,0:T(8,128)(2,1)}, bf16[1024,256]{1,0:T(8,128)(2,1)S(1)}, u32[]{:S(2)}, u32[]{:S(2)}) collective-permute-start(bf16[1024,256]{1,0:T(8,128)(2,1)} %get-tuple-element.50.refs_0_.refs_2_), channel_id=1, source_target_pairs={{0,48},{16,0},{32,16},{48,32},{64,112},{80,64},{96,80},{112,96},{1... | collective-permute-start | bytes 1572872 | tf_op jit(solution)/shard_map/ppermute | solution.py:506
  11.9 22.0 %collective-permute-start.3 = (bf16[1024,256]{1,0:T(8,128)(2,1)}, bf16[1024,256]{1,0:T(8,128)(2,1)S(1)}, u32[]{:S(2)}, u32[]{:S(2)}) collective-permute-start(bf16[1024,256]{1,0:T(8,128)(2,1)} %get-tuple-element.50.refs_0_.refs_2_), channel_id=1, source_target_pairs={{0,16},{16,32},{32,48},{48,0},{64,80},{80,96},{96,112},{112,64},{1... | collective-permute-start | bytes 1572872 | tf_op jit(solution)/shard_map/ppermute | solution.py:506
  14.8 21.6 %collective-permute-start.1 = (bf16[1024,256]{1,0:T(8,128)(2,1)S(1)}, bf16[1024,256]{1,0:T(8,128)(2,1)S(1)}, u32[]{:S(2)}, u32[]{:S(2)}) collective-permute-start(bf16[1024,256]{1,0:T(8,128)(2,1)S(1)} %get-tuple-element.51.refs_1_.refs_2_.refs_3_), channel_id=1, source_target_pairs={{0,64},{16,80},{32,96},{48,112},{64,0},{80,16},{96,32},{112,48},{1... | collective-permute-start | bytes 1572872 | tf_op jit(solution)/shard_map/ppermute | solution.py:509
  17.7 22.4 %collective-permute-start = (bf16[1024,256]{1,0:T(8,128)(2,1)S(1)}, bf16[1024,256]{1,0:T(8,128)(2,1)S(1)}, u32[]{:S(2)}, u32[]{:S(2)}) collective-permute-start(bf16[1024,256]{1,0:T(8,128)(2,1)S(1)} %copy-done.4), channel_id=1, source_target_pairs={{0,32},{16,48},{32,0},{48,16},{64,96},{80,112},{96,64},{112,80},{1... | collective-permute-start | bytes 1572872 | tf_op jit(solution)/shard_map/ppermute | solution.py:506
  19.0 17.5 %collective-permute-start.2 = (f32[2,1024]{1,0:T(2,128)S(1)}, f32[2,1024]{1,0:T(2,128)S(1)}, u32[]{:S(2)}, u32[]{:S(2)}) collective-permute-start(f32[2,1024]{1,0:T(2,128)S(1)} %copy-done.7), channel_id=1, source_target_pairs={{0,64},{16,80},{32,96},{48,112},{64,0},{80,16},{96,32},{112,48},{1... | collective-permute-start | bytes 24584 | tf_op jit(solution)/shard_map/ppermute | solution.py:509
  42.5 4.4 %collective-permute-start.5 = (f32[4,1024]{1,0:T(4,128)S(1)}, f32[4,1024]{1,0:T(4,128)S(1)}, u32[]{:S(2)}, u32[]{:S(2)}) collective-permute-start(f32[4,1024]{1,0:T(4,128)S(1)} %get-tuple-element.56.refs_0_), channel_id=1, source_target_pairs={{0,64},{16,80},{32,96},{48,112},{64,0},{80,16},{96,32},{112,48},{1... | collective-permute-start | bytes 49160 | tf_op jit(solution)/shard_map/ppermute | solution.py:509
  52.8 11.6 %collective-permute-start.6 = (bf16[256,1024]{1,0:T(8,128)(2,1)S(1)}, bf16[256,1024]{1,0:T(8,128)(2,1)S(1)}, u32[]{:S(2)}, u32[]{:S(2)}) collective-permute-start(bf16[256,1024]{1,0:T(8,128)(2,1)S(1)} %get-tuple-element.73), channel_id=1, source_target_pairs={{0,64},{16,80},{32,96},{48,112},{64,0},{80,16},{96,32},{112,48},{1... | collective-permute-start | bytes 1572872 | tf_op jit(solution)/shard_map/ppermute | solution.py:509
  58.4 14.5 %collective-permute-start.10 = (bf16[1024,256]{1,0:T(8,128)(2,1)S(1)}, bf16[1024,256]{1,0:T(8,128)(2,1)S(1)}, u32[]{:S(2)}, u32[]{:S(2)}) collective-permute-start(bf16[1024,256]{1,0:T(8,128)(2,1)S(1)} %get-tuple-element.82), channel_id=1, source_target_pairs={{0,16},{16,32},{32,48},{48,0},{64,80},{80,96},{96,112},{112,64},{1... | collective-permute-start | bytes 1572872 | tf_op jit(solution)/shard_map/ppermute | solution.py:506
  58.4 15.3 %collective-permute-start.9 = (bf16[1024,256]{1,0:T(8,128)(2,1)S(1)}, bf16[1024,256]{1,0:T(8,128)(2,1)S(1)}, u32[]{:S(2)}, u32[]{:S(2)}) collective-permute-start(bf16[1024,256]{1,0:T(8,128)(2,1)S(1)} %get-tuple-element.81), channel_id=1, source_target_pairs={{0,48},{16,0},{32,16},{48,32},{64,112},{80,64},{96,80},{112,96},{1... | collective-permute-start | bytes 1572872 | tf_op jit(solution)/shard_map/ppermute | solution.py:506
  62.0 21.4 %collective-permute-start.8 = (bf16[1024,256]{1,0:T(8,128)(2,1)S(1)}, bf16[1024,256]{1,0:T(8,128)(2,1)S(1)}, u32[]{:S(2)}, u32[]{:S(2)}) collective-permute-start(bf16[1024,256]{1,0:T(8,128)(2,1)S(1)} %get-tuple-element.80), channel_id=1, source_target_pairs={{0,32},{16,48},{32,0},{48,16},{64,96},{80,112},{96,64},{112,80},{1... | collective-permute-start | bytes 1572872 | tf_op jit(solution)/shard_map/ppermute | solution.py:506
  64.4 18.9 %copy-start = (bf16[1024,1024]{1,0:T(8,128)(2,1)S(1)}, bf16[1024,1024]{1,0:T(8,128)(2,1)}, u32[]{:S(2)}) copy-start(bf16[1024,1024]{1,0:T(8,128)(2,1)} %refs_0_.3) | copy-start | bytes 6291460
  64.4 18.9 %copy-start.2 = (bf16[1024,512]{1,0:T(8,128)(2,1)S(1)}, bf16[1024,512]{1,0:T(8,128)(2,1)}, u32[]{:S(2)}) copy-start(bf16[1024,512]{1,0:T(8,128)(2,1)} %get-tuple-element.77.refs_2_) | copy-start | bytes 3145732
  64.4 18.9 %copy-start.3 = (f32[1024,256]{1,0:T(8,128)S(1)}, f32[1024,256]{1,0:T(8,128)}, u32[]{:S(2)}) copy-start(f32[1024,256]{1,0:T(8,128)} %get-tuple-element.78.refs_3_) | copy-start | bytes 3145732
  64.5 18.9 %copy-start.5 = (bf16[512,256]{1,0:T(8,128)(2,1)S(1)}, bf16[512,256]{1,0:T(8,128)(2,1)}, u32[]{:S(2)}) copy-start(bf16[512,256]{1,0:T(8,128)(2,1)} %refs_1_.3) | copy-start | bytes 786436
  67.5 24.3 %collective-permute-start.7 = (bf16[2568,128]{1,0:T(8,128)(2,1)S(1)}, bf16[2568,128]{1,0:T(8,128)(2,1)S(1)}, u32[]{:S(2)}, u32[]{:S(2)}) collective-permute-start(bf16[2568,128]{1,0:T(8,128)(2,1)S(1)} %get-tuple-element.76), channel_id=1, source_target_pairs={{0,1},{1,0},{2,3},{3,2},{4,5},{5,4},{6,7},{7,6},{8,9},{9,8},{10,11... | collective-permute-start | bytes 1972232 | tf_op jit(solution)/shard_map/ppermute | solution.py:512
  86.2 5.6 %collective-permute-start.11 = (bf16[2560,128]{1,0:T(8,128)(2,1)S(1)}, bf16[2560,128]{1,0:T(8,128)(2,1)S(1)}, u32[]{:S(2)}, u32[]{:S(2)}) collective-permute-start(bf16[2560,128]{1,0:T(8,128)(2,1)S(1)} %get-tuple-element.84), channel_id=1, source_target_pairs={{0,1},{1,0},{2,3},{3,2},{4,5},{5,4},{6,7},{7,6},{8,9},{9,8},{10,11... | collective-permute-start | bytes 1966088 | tf_op jit(solution)/shard_map/ppermute | solution.py:512
  147.0 5.2 %collective-permute-start.12 = (bf16[64,80,128]{2,1,0:T(8,128)(2,1)S(1)}, bf16[64,80,128]{2,1,0:T(8,128)(2,1)S(1)}, u32[]{:S(2)}, u32[]{:S(2)}) collective-permute-start(bf16[64,80,128]{2,1,0:T(8,128)(2,1)S(1)} %all_to_all.11.mine), channel_id=1, source_target_pairs={{0,1},{1,0},{2,3},{3,2},{4,5},{5,4},{6,7},{7,6},{8,9},{9,8},{10,11... | collective-permute-start | bytes 3932168 | tf_op jit(solution)/shard_map/ppermute | solution.py:512
where the time goes:
time: 155 us
  blocking collectives  53.6 us (35%)
  Pallas kernels  39.7 us (26%)
  starting transfers between devices  31.3 us (20%)
  waiting for transfers between devices  29.7 us (19%)
    all_to_all x1, blocking collectives, sum_over_all(): parts = lax.all_to_all(to_sum, peers, 0, 0, tiled=True)  28.8 us
    all_to_all x1, blocking collectives, sum_over_all(): mine = lax.all_to_all(to_share, peers, 0, 0, tiled=True)  24.8 us
    ppermute x6, waiting for transfers between devices, along_z(): return lax.ppermute(value, 'row', pairs)  23.9 us
    ppermute x3, starting transfers between devices, other_core(): return lax.ppermute(value, 'core', [(0, 1), (1, 0)])  11.8 us
    ppermute x6, starting transfers between devices, along_z(): return lax.ppermute(value, 'row', pairs)  10.6 us
    pallas_call x5, Pallas kernels, vector_grads(): pl.pallas_call(functools.partial(vectors_kernel, plan, unit), in_specs=in...  9.98 us
    pallas_call x4, Pallas kernels, scores(): pl.pallas_call(functools.partial(scores_kernel, blocks, len(items), len(u...  9.82 us
    ppermute x4, starting transfers between devices, partner(): lax.ppermute(value, 'row', [(k, (k + NZ) % n_row) for k in range(n_row)])  8.91 us
  transfers between devices with their start and end apart: 13, of which 6 were waited for; matrix products, arithmetic and copies ran while one was open for 0% of the time, Pallas kernels for 13%

commit v1 on v0

--- a/solution.py
+++ b/solution.py
@@ -34,108 +34,114 @@
     return pltpu.CompilerParams(vmem_limit_bytes=mib * 2**20)
 
 
-def whole(shape):
-    return pl.BlockSpec(shape, lambda *_: (0,) * len(shape))
-
-
 def in_vmem(n):
     return [pl.BlockSpec(memory_space=pltpu.VMEM)] * n
 
 
-def forward_kernel(feats, first, second, vec, hidden, out):
-    pre = dot(feats[...], first[...])
-    h = jnp.maximum(pre, 0.0).astype(BF)
-    hidden[...] = h
-    o = dot(h, second[...])
-    out[...] = o
-    inv = lax.rsqrt(jnp.mean(o * o, axis=-1, keepdims=True) + EPS)
-    vec[...] = (o * inv).astype(BF)
+def forward_of(feats, first, second):
+    h = jnp.maximum(dot(feats, first), 0.0).astype(BF)
+    out = dot(h, second)
+    inv = lax.rsqrt(jnp.mean(out * out, axis=-1, keepdims=True) + EPS)
+    return (out * inv).astype(BF), h, out
+
+
+def forward_kernel(feats, first, second, *results):
+    def step(k, carry):
+        for r in range(0, 2 * ROWS, ROWS):
+            here = pl.ds(pl.multiple_of(k * 2 * ROWS + r, ROWS), ROWS)
+            for ref, value in zip(results, forward_of(feats[here, :], first[...], second[...])):
+                ref[here, :] = value
+        return carry
+
+    lax.fori_loop(0, feats.shape[0] // (2 * ROWS), step, 0)
+
+
+def forward_shapes(m, hid, emb):
+    return [((m, emb), BF), ((m, hid), BF), ((m, emb), F32)]
+
+
+def forward_cost(m, f, hid, emb):
+    return cost(2 * m * hid * (f + emb), 2 * m * f + 2 * f * hid + 6 * m * emb)
 
 
 def tower_forward(feats, first, second):
-    m, f = feats.shape
-    hid, emb = second.shape
+    shapes = forward_shapes(feats.shape[0], *second.shape)
     return pl.pallas_call(
         forward_kernel,
-        grid=(m // ROWS,),
-        in_specs=[
-            pl.BlockSpec((ROWS, f), lambda i: (i, 0)),
-            whole(first.shape),
-            whole(second.shape),
-        ],
-        out_specs=[
-            pl.BlockSpec((ROWS, emb), lambda i: (i, 0)),
-            pl.BlockSpec((ROWS, hid), lambda i: (i, 0)),
-            pl.BlockSpec((ROWS, emb), lambda i: (i, 0)),
-        ],
-        out_shape=[
-            jax.ShapeDtypeStruct((m, emb), BF),
-            jax.ShapeDtypeStruct((m, hid), BF),
-            jax.ShapeDtypeStruct((m, emb), F32),
-        ],
-        cost_estimate=cost(2 * m * hid * (f + emb), 2 * m * f + 2 * f * hid + 6 * m * emb),
+        in_specs=in_vmem(3),
+        out_specs=in_vmem(3),
+        out_shape=[jax.ShapeDtypeStruct(*s) for s in shapes],
+        cost_estimate=forward_cost(*feats.shape, *second.shape),
         compiler_params=grant(10),
         name="tower_forward",
     )(feats, first, second)
 
 
-def first_forward_kernel(feats, first, second, sharp, chosen, vec, hidden, out, meta, x, w1, w2, sems):
+def first_forward_kernel(steps, *refs):
+    feats, first, second, sharp, chosen = refs[:5]
+    results_out, meta_out = refs[5:8], refs[8]
+    x, w1, w2, sharp_in, chosen_in, meta = refs[9:15]
+    results, sems, out_sems = refs[15:18], refs[18], refs[19]
+    blocks = [pl.ds(k * ROWS, ROWS) for k in range(steps)]
+    copy = pltpu.make_async_copy
+    feats_in = [copy(feats.at[here], x.at[here], sems.at[k]) for k, here in enumerate(blocks)]
+    half = first.shape[0] // 2
+    weights_in = [copy(second, w2, sems.at[steps])]
+    for k in range(2):
+        here = pl.ds(k * half, half)
+        weights_in.append(copy(first.at[here], w1.at[here], sems.at[steps + 1 + k]))
+    rows_in = [
+        copy(sharp, sharp_in, sems.at[steps + 3]),
+        copy(chosen, chosen_in, sems.at[steps + 4]),
+    ]
+    for one in (feats_in[0], *weights_in, *feats_in[1:], *rows_in):
+        one.start()
+    copies = []
+    for one in weights_in:
+        one.wait()
+    for k in range(steps):
+        feats_in[k].wait()
+        here = blocks[k]
+        values = forward_of(x[here, :], w1[...], w2[...])
+        for j in range(3):
+            results[j][here, :] = values[j]
+            copies.append(copy(results[j].at[here], results_out[j].at[here], out_sems.at[j, k]))
+            copies[-1].start()
+        if k == 0:
+            for one in rows_in:
+                one.wait()
+            for which, rows in enumerate((sharp_in[...].astype(F32), chosen_in[...].astype(F32))):
+                for i in range(rows.shape[0]):
+                    meta[which : which + 1, i * LANES : (i + 1) * LANES] = rows[i : i + 1, :]
+            copies.append(copy(meta, meta_out, out_sems.at[3, 0]))
+            copies[-1].start()
+    for one in copies:
+        one.wait()
+
+
+def first_tower_forward(feats, first, second, sharp, chosen):
     m, f = feats.shape
     steps = m // ROWS
-    slices = [pl.ds(k * ROWS, ROWS) for k in range(steps)]
-    halves = [pl.ds(k * (f // 2), f // 2) for k in range(2)]
-    copies = [
-        pltpu.make_async_copy(feats.at[slices[0]], x.at[slices[0]], sems.at[0]),
-        pltpu.make_async_copy(first.at[halves[0]], w1.at[halves[0]], sems.at[1]),
-        pltpu.make_async_copy(first.at[halves[1]], w1.at[halves[1]], sems.at[2]),
-        pltpu.make_async_copy(second, w2, sems.at[3]),
-    ]
-    copies += [
-        pltpu.make_async_copy(feats.at[slices[k]], x.at[slices[k]], sems.at[3 + k])
-        for k in range(1, steps)
-    ]
-    for copy in copies:
-        copy.start()
-    for which, rows in enumerate((sharp[...].astype(F32), chosen[...].astype(F32))):
-        for k in range(rows.shape[0]):
-            meta[which : which + 1, k * LANES : (k + 1) * LANES] = rows[k : k + 1, :]
-    for copy in copies[:4]:
-        copy.wait()
-    for k in range(steps):
-        if k:
-            copies[3 + k].wait()
-        here = slice(k * ROWS, (k + 1) * ROWS)
-        h = jnp.maximum(dot(x[here, :], w1[...]), 0.0).astype(BF)
-        hidden[here, :] = h
-        o = dot(h, w2[...])
-        out[here, :] = o
-        inv = lax.rsqrt(jnp.mean(o * o, axis=-1, keepdims=True) + EPS)
-        vec[here, :] = (o * inv).astype(BF)
-
-
-def first_tower_forward(feats, first, second, sharp, chosen):
-    m, f = feats.shape
-    hid, emb = second.shape
+    results = [*forward_shapes(m, *second.shape), ((2, m), F32)]
+    sharp, chosen = sharp.reshape(-1, LANES), chosen.reshape(-1, LANES)
+    operands = (feats, first, second, sharp, chosen)
+    in_hbm = pl.BlockSpec(memory_space=pltpu.HBM)
     return pl.pallas_call(
-        first_forward_kernel,
-        in_specs=[pl.BlockSpec(memory_space=pltpu.HBM)] * 3 + in_vmem(2),
-        out_specs=in_vmem(4),
-        out_shape=[
-            jax.ShapeDtypeStruct((m, emb), BF),
-            jax.ShapeDtypeStruct((m, hid), BF),
-            jax.ShapeDtypeStruct((m, emb), F32),
-            jax.ShapeDtypeStruct((2, m), F32),
+        functools.partial(first_forward_kernel, steps),
+        in_specs=[in_hbm] * 5,
+        out_specs=[in_hbm] * 4,
+        out_shape=[jax.ShapeDtypeStruct(*s) for s in results],
+        scratch_shapes=[
+            *[pltpu.VMEM(x.shape, x.dtype) for x in operands],
+            pltpu.VMEM(*results[3]),
+            *[pltpu.VMEM(*s) for s in results[:3]],
+            pltpu.SemaphoreType.DMA((steps + 5,)),
+            pltpu.SemaphoreType.DMA((4, steps)),
         ],
-        scratch_shapes=[
-            pltpu.VMEM((m, f), BF),
-            pltpu.VMEM((f, hid), BF),
-            pltpu.VMEM((hid, emb), BF),
-            pltpu.SemaphoreType.DMA((3 + m // ROWS,)),
-        ],
-        cost_estimate=cost(2 * m * hid * (f + emb), 2 * m * f + 2 * f * hid + 6 * m * emb),
+        cost_estimate=forward_cost(m, f, *second.shape),
         compiler_params=grant(58),
         name="tower_forward",
-    )(feats, first, second, sharp.reshape(-1, LANES), chosen.reshape(-1, LANES))
+    )(*operands)
 
 
 def first_item(slot, rows):
@@ -327,7 +333,7 @@
         loss, refs = refs[0], refs[1:]
     kept, sent, grad_out, grad_pre, first, last = refs
     m, f = feats.shape
-    hid, _ = second.shape
+    hid, emb = second.shape
     for r in range(0, m, ROWS):
         here = slice(r, r + ROWS)
         at = (slice(None), here) if turned else (here, slice(None))
@@ -347,38 +353,25 @@
         grad_pre[here, :] = jnp.where(hidden[here, :] > 0, back, 0.0).astype(BF)
     for r in range(0, hid, ROWS):
         here = slice(r, r + ROWS)
-        last[here, :] = dot(hidden[:, here], grad_out[...], (0, 0)).astype(BF)
+        part = dot(hidden[:, here], grad_out[...], (0, 0)).astype(BF)
+        for k in range(emb // LANES):
+            last[k, here, :] = part[:, k * LANES : (k + 1) * LANES]
     for r in range(0, f, ROWS):
         here = slice(r, r + ROWS)
-        first[here, :] = dot(feats[:, here], grad_pre[...], (0, 0)).astype(BF)
+        part = dot(feats[:, here], grad_pre[...], (0, 0)).astype(BF)
+        for k in range(hid // LANES):
+            first[k, here, :] = part[:, k * LANES : (k + 1) * LANES]
     core = lax.axis_index("core")
     half = kept.shape[0]
-    for which in range(2):
-
-        @pl.when(core == which)
-        def _():
-            targets = (sent, kept) if which else (kept, sent)
-            for array, k, start, rows, place, at in pieces(first, last, half):
-                targets[place][at : at + rows, :] = array[
-                    start : start + rows, k * LANES : (k + 1) * LANES
-                ]
-
+    for target, whose in ((kept, core), (sent, 1 - core)):
+        at = 0
+        for array in (first, last):
+            groups, rows, _ = array.shape
+            for k in range(groups // 2):
+                target[at : at + rows, :] = array[whose * (groups // 2) + k]
+                at += rows
     if has_loss:
         sent[half : half + 8, :] = three_terms(loss[...]).astype(BF)
-
-
-def pieces(first, second, half):
-    at = 0
-    for array in (first, second):
-        rows, cols = array.shape
-        for k in range(cols // LANES):
-            done = 0
-            while done < rows:
-                place, inside = divmod(at, half)
-                take = min(rows - done, half - inside)
-                yield array, k, done, take, place, inside
-                done += take
-                at += take
 
 
 def tower_backward(feats, second, hidden, out, own, others, turned, loss=None):
@@ -396,8 +389,8 @@
         scratch_shapes=[
             pltpu.VMEM((m, emb), BF),
             pltpu.VMEM((m, hid), BF),
-            pltpu.VMEM((f, hid), BF),
-            pltpu.VMEM((hid, emb), BF),
+            pltpu.VMEM((hid // LANES, f, LANES), BF),
+            pltpu.VMEM((emb // LANES, hid, LANES), BF),
         ],
         cost_estimate=cost(2 * m * hid * (f + 2 * emb), 2 * m * f + 4 * f * hid + 10 * m * emb),
         compiler_params=grant(12),
@@ -426,25 +419,53 @@
         out[k] = summed
 
 
-def unpack_kernel(mine, theirs, *outs):
-    n_peers, rows, _ = mine.shape
+def unpack_kernel(is_mine, *refs):
+    half = refs[0]
+    outs, stages, sems = refs[-9:-5], refs[-5:-1], refs[-1]
+    n_peers, rows, _ = half.shape
     share = rows // 2
-    half = n_peers * share
     core = lax.axis_index("core")
-    for which in range(2):
-
-        @pl.when(core == which)
-        def _():
-            halves = (theirs, mine) if which else (mine, theirs)
-            for tower in range(2):
-                values = [
-                    x[:, tower * share : (tower + 1) * share, :].reshape(half, LANES) for x in halves
-                ]
-                first, second = outs[2 * tower : 2 * tower + 2]
-                for out, k, start, count, place, at in pieces(first, second, half):
-                    out[start : start + count, k * LANES : (k + 1) * LANES] = values[place][
-                        at : at + count, :
+    whose = core if is_mine else 1 - core
+    copies = []
+    for tower in range(2):
+        value = half[:, tower * share : (tower + 1) * share, :].reshape(n_peers * share, LANES)
+        base = 0
+        for which in (2 * tower, 2 * tower + 1):
+            count, cols = stages[which].shape
+            columns = pl.ds(pl.multiple_of(whose * cols, cols), cols)
+            for r in range(0, count, 2 * ROWS):
+                here = pl.ds(r, 2 * ROWS)
+                for k in range(cols // LANES):
+                    at = base + k * count + r
+                    stages[which][here, k * LANES : (k + 1) * LANES] = value[
+                        at : at + 2 * ROWS
                     ].astype(F32)
+                copy = pltpu.make_async_copy(
+                    stages[which].at[here], outs[which].at[here, columns], sems.at[len(copies)]
+                )
+                copy.start()
+                copies.append(copy)
+            base += count * cols // LANES
+    for copy in copies:
+        copy.wait()
+
+
+def unpack(half, shapes, so_far=()):
+    in_hbm = pl.BlockSpec(memory_space=pltpu.HBM)
+    return pl.pallas_call(
+        functools.partial(unpack_kernel, not so_far),
+        in_specs=in_vmem(1) + [in_hbm] * len(so_far),
+        out_specs=[in_hbm] * 4,
+        out_shape=[jax.ShapeDtypeStruct(s, F32) for s in shapes],
+        input_output_aliases={1 + k: k for k in range(len(so_far))},
+        scratch_shapes=[
+            *[pltpu.VMEM((s[0], s[1] // 2), F32) for s in shapes],
+            pltpu.SemaphoreType.DMA((sum(s[0] // (2 * ROWS) for s in shapes),)),
+        ],
+        cost_estimate=cost(10**8, 3 * half.size),
+        compiler_params=grant(10),
+        name="unpack",
+    )(half, *so_far)
 
 
 def sum_over_all(user_parts, item_parts, loss, shapes, other_core, count):
@@ -475,14 +496,8 @@
     )(parts)
     mine = lax.all_to_all(to_share, peers, 0, 0, tiled=True)
     theirs = other_core(mine)
-    grads = pl.pallas_call(
-        unpack_kernel,
-        in_specs=in_vmem(2),
-        out_specs=in_vmem(4),
-        out_shape=[jax.ShapeDtypeStruct(s, F32) for s in shapes],
-        compiler_params=grant(14),
-        name="unpack",
-    )(mine, theirs)
+    grads = unpack(mine, shapes)
+    grads = unpack(theirs, shapes, tuple(grads))
     return (loss.reshape(()), *grads)
 
 

time: 155 us -> 153 us (0.987)
    pallas_call x3 -> x4, Pallas kernels: 12.5 us -> 10.9 us  [the longest x1 5.51 us: first_tower_forward(): pl.pallas_call(functools.partial(first_forward_kernel, steps), in_specs=[...]
    ppermute x3, waiting for transfers between devices: 4.39 us -> 2.82 us  [other_core(): return lax.ppermute(value, 'core', [(0, 1), (1, 0)])]
  transfers between devices with their start and end apart: 13 -> 13, of which waited for: 6 -> 6; matrix products, arithmetic and copies ran while one was open for 0% -> 0% of each run, Pallas kernels for 13% -> 14%
where the time goes in v1:
time: 153 us
  blocking collectives  53.6 us (35%)
  Pallas kernels  38.2 us (25%)
  starting transfers between devices  31.3 us (20%)
  waiting for transfers between devices  28.6 us (19%)
    all_to_all x1, blocking collectives, sum_over_all(): parts = lax.all_to_all(to_sum, peers, 0, 0, tiled=True)  28.8 us
    all_to_all x1, blocking collectives, sum_over_all(): mine = lax.all_to_all(to_share, peers, 0, 0, tiled=True)  24.8 us
    ppermute x6, waiting for transfers between devices, along_z(): return lax.ppermute(value, 'row', pairs)  24.4 us
    ppermute x3, starting transfers between devices, other_core(): return lax.ppermute(value, 'core', [(0, 1), (1, 0)])  11.8 us
    ppermute x6, starting transfers between devices, along_z(): return lax.ppermute(value, 'row', pairs)  10.6 us
    pallas_call x5, Pallas kernels, vector_grads(): pl.pallas_call(functools.partial(vectors_kernel, plan, unit), in_specs=in...  9.98 us
    pallas_call x4, Pallas kernels, scores(): pl.pallas_call(functools.partial(scores_kernel, blocks, len(items), len(u...  9.82 us
    ppermute x4, starting transfers between devices, partner(): lax.ppermute(value, 'row', [(k, (k + NZ) % n_row) for k in range(n_row)])  8.91 us
  transfers between devices with their start and end apart: 13, of which 6 were waited for; matrix products, arithmetic and copies ran while one was open for 0% of the time, Pallas kernels for 14%

profile of v1, /device:TPU:1, one launch (start us, length us, event | category | flops | bytes accessed | tf_op | source)
XLA Modules:
  0.0 152.9 jit_solution(10667361216913161740)
XLA Ops:
  0.7 5.5 %tower_forward.3 = (bf16[1024,256]{1,0:T(8,128)(2,1)}, bf16[1024,512]{1,0:T(8,128)(2,1)}, f32[1024,256]{1,0:T(8,128)}, f32[2,1024]{1,0:T(2,128)}) custom-call(bf16[1024,1024]{1,0:T(8,128)(2,1)} %refs_0_.5, bf16[1024,512]{1,0:T(8,128)(2,1)} %refs_1_.3, bf16[512,256]{1,0:T(8,128)(2,1)} %refs_1_.5, bf16[8,128]{1,0:T(8,128)(2,1)} %bitcast.4, s32[8,128]{1,0:T(8,128)} %bitcast.3), custom_call_target="tpu_custom_call" | custom-call | flops 1342177280 | bytes 4718592 | tf_op jit(solution)/shard_map/tower_forward/pallas_call | solution.py:129
  6.2 4.6 %collective-permute-start.4 = (bf16[1024,256]{1,0:T(8,128)(2,1)}, bf16[1024,256]{1,0:T(8,128)(2,1)S(1)}, u32[]{:S(2)}, u32[]{:S(2)}) collective-permute-start(bf16[1024,256]{1,0:T(8,128)(2,1)} %get-tuple-element.54.refs_0_.refs_2_), channel_id=1, source_target_pairs={{0,48},{16,0},{32,16},{48,32},{64,112},{80,64},{96,80},{112,96},{1... | collective-permute-start | bytes 1572872 | tf_op jit(solution)/shard_map/ppermute | solution.py:521
  10.9 2.2 %tower_forward.2 = (bf16[1024,256]{1,0:T(8,128)(2,1)S(1)}, bf16[1024,512]{1,0:T(8,128)(2,1)S(1)}, f32[1024,256]{1,0:T(8,128)S(1)}) custom-call(bf16[1024,1024]{1,0:T(8,128)(2,1)S(1)} %copy-done.1, bf16[1024,512]{1,0:T(8,128)(2,1)S(1)} %copy-done.8, bf16[512,256]{1,0:T(8,128)(2,1)S(1)} %copy-done.6), custom_call_target="tpu_custom_call" | custom-call | flops 1342177280 | bytes 4718592 | tf_op jit(solution)/shard_map/tower_forward/pallas_call | solution.py:69
  13.1 2.8 %collective-permute-start.1 = (bf16[1024,256]{1,0:T(8,128)(2,1)S(1)}, bf16[1024,256]{1,0:T(8,128)(2,1)S(1)}, u32[]{:S(2)}, u32[]{:S(2)}) collective-permute-start(bf16[1024,256]{1,0:T(8,128)(2,1)S(1)} %get-tuple-element.55.refs_1_.refs_2_.refs_3_), channel_id=1, source_target_pairs={{0,64},{16,80},{32,96},{48,112},{64,0},{80,16},{96,32},{112,48},{1... | collective-permute-start | bytes 1572872 | tf_op jit(solution)/shard_map/ppermute | solution.py:524
  18.8 14.1 %collective-permute-done.4.refs_1_.refs_2_.refs_4_ = bf16[1024,256]{1,0:T(8,128)(2,1)S(1)} collective-permute-done((bf16[1024,256]{1,0:T(8,128)(2,1)}, bf16[1024,256]{1,0:T(8,128)(2,1)S(1)}, u32[]{:S(2)}, u32[]{:S(2)}) %collective-permute-start.4) | collective-permute-done | bytes 524320 | tf_op jit(solution)/shard_map/ppermute | solution.py:521
  32.9 2.5 %scores.5 = (bf16[1024,1024]{1,0:T(8,128)(2,1)S(1)}, bf16[1024,1024]{1,0:T(8,128)(2,1)S(1)}, f32[2,1024]{1,0:T(2,128)S(1)}) custom-call(bf16[1024,256]{1,0:T(8,128)(2,1)S(1)} %collective-permute-done.3.refs_0_.refs_1_.refs_3_.refs_2_, bf16[1024,256]{1,0:T(8,128)(2,1)S(1)} %collective-permute-done.4.refs_1_.refs_2_.refs_4_, ...), custom_call_target="tpu_custom_call" | custom-call | flops 1073741824 | bytes 4194304 | tf_op jit(solution)/shard_map/scores/pallas_call | solution.py:200
  35.4 3.6 %scores.6 = (bf16[1024,1024]{1,0:T(8,128)(2,1)S(1)}, bf16[1024,1024]{1,0:T(8,128)(2,1)S(1)}, bf16[1024,1024]{1,0:T(8,128)(2,1)S(1)}, f32[2,1024]{1,0:T(2,128)S(1)}) custom-call(bf16[1024,256]{1,0:T(8,128)(2,1)S(1)} %copy-done.4, bf16[1024,256]{1,0:T(8,128)(2,1)S(1)} %collective-permute-done.3.refs_0_.refs_1_.refs_3_.refs_2_, ...), custom_call_target="tpu_custom_call" | custom-call | flops 1610612736 | bytes 6291456 | tf_op jit(solution)/shard_map/scores/pallas_call | solution.py:200
  39.0 2.4 %scores.7 = (bf16[1024,1024]{1,0:T(8,128)(2,1)S(1)}, bf16[1024,1024]{1,0:T(8,128)(2,1)S(1)}, f32[4,1024]{1,0:T(4,128)S(1)}) custom-call(bf16[1024,256]{1,0:T(8,128)(2,1)S(1)} %collective-permute-done.refs_0_.refs_2_, bf16[1024,256]{1,0:T(8,128)(2,1)S(1)} %get-tuple-element.55.refs_1_.refs_2_.refs_3_, ...), custom_call_target="tpu_custom_call" | custom-call | flops 1073741824 | bytes 4194304 | tf_op jit(solution)/shard_map/scores/pallas_call | solution.py:200
  41.4 3.0 %collective-permute-start.5 = (f32[4,1024]{1,0:T(4,128)S(1)}, f32[4,1024]{1,0:T(4,128)S(1)}, u32[]{:S(2)}, u32[]{:S(2)}) collective-permute-start(f32[4,1024]{1,0:T(4,128)S(1)} %get-tuple-element.60.refs_0_), channel_id=1, source_target_pairs={{0,64},{16,80},{32,96},{48,112},{64,0},{80,16},{96,32},{112,48},{1... | collective-permute-start | bytes 49160 | tf_op jit(solution)/shard_map/ppermute | solution.py:524
  45.8 2.4 %vector_grads.5 = (bf16[1024,256]{1,0:T(8,128)(2,1)S(1)}, f32[256,1024]{1,0:T(8,128)S(1)}, f32[256,1024]{1,0:T(8,128)S(1)}) custom-call(f32[4,1024]{1,0:T(4,128)S(1)} %get-tuple-element.60.refs_0_, f32[4,1024]{1,0:T(4,128)S(1)} %collective-permute-done.5.refs_1_, bf16[1024,256]{1,0:T(8,128)(2,1)S(1)} %collective-permute-done.refs_0_.refs_2_, ...), custom_call_target="tpu_custom_call" | custom-call | flops 2147483648 | bytes 6815744 | tf_op jit(solution)/shard_map/vector_grads/pallas_call | solution.py:310
  48.2 3.5 %vector_grads.6 = (f32[1024,256]{1,0:T(8,128)S(1)}, f32[1024,256]{1,0:T(8,128)S(1)}, f32[1024,256]{1,0:T(8,128)S(1)}, bf16[256,1024]{1,0:T(8,128)(2,1)S(1)}) custom-call(f32[4,1024]{1,0:T(4,128)S(1)} %get-tuple-element.60.refs_0_, f32[4,1024]{1,0:T(4,128)S(1)} %collective-permute-done.5.refs_1_, bf16[1024,256]{1,0:T(8,128)(2,1)S(1)} %copy-done.4, ...), custom_call_target="tpu_custom_call" | custom-call | flops 3221225472 | bytes 8912896 | tf_op jit(solution)/shard_map/vector_grads/pallas_call | solution.py:310
  51.8 2.8 %collective-permute-start.6 = (bf16[256,1024]{1,0:T(8,128)(2,1)S(1)}, bf16[256,1024]{1,0:T(8,128)(2,1)S(1)}, u32[]{:S(2)}, u32[]{:S(2)}) collective-permute-start(bf16[256,1024]{1,0:T(8,128)(2,1)S(1)} %get-tuple-element.77), channel_id=1, source_target_pairs={{0,64},{16,80},{32,96},{48,112},{64,0},{80,16},{96,32},{112,48},{1... | collective-permute-start | bytes 1572872 | tf_op jit(solution)/shard_map/ppermute | solution.py:524
  57.4 3.5 %collective-permute-start.9 = (bf16[1024,256]{1,0:T(8,128)(2,1)S(1)}, bf16[1024,256]{1,0:T(8,128)(2,1)S(1)}, u32[]{:S(2)}, u32[]{:S(2)}) collective-permute-start(bf16[1024,256]{1,0:T(8,128)(2,1)S(1)} %get-tuple-element.85), channel_id=1, source_target_pairs={{0,48},{16,0},{32,16},{48,32},{64,112},{80,64},{96,80},{112,96},{1... | collective-permute-start | bytes 1572872 | tf_op jit(solution)/shard_map/ppermute | solution.py:521
  63.4 3.2 %tower_backward.2 = (bf16[2560,128]{1,0:T(8,128)(2,1)S(1)}, bf16[2568,128]{1,0:T(8,128)(2,1)S(1)}) custom-call(bf16[1024,1024]{1,0:T(8,128)(2,1)S(1)} %copy-done.1, bf16[512,256]{1,0:T(8,128)(2,1)S(1)} %copy-done.6, bf16[1024,512]{1,0:T(8,128)(2,1)S(1)} %get-tuple-element.52.refs_2_, f32[1024,256]{1,0:T(8,128)S(1)} %get-tuple-element.53.refs_3_, ...), custom_call_target="tpu_custom_call" | custom-call | flops 1610612736 | bytes 6815744 | tf_op jit(solution)/shard_map/tower_backward/pallas_call | solution.py:384
  66.6 5.4 %collective-permute-start.7 = (bf16[2568,128]{1,0:T(8,128)(2,1)S(1)}, bf16[2568,128]{1,0:T(8,128)(2,1)S(1)}, u32[]{:S(2)}, u32[]{:S(2)}) collective-permute-start(bf16[2568,128]{1,0:T(8,128)(2,1)S(1)} %get-tuple-element.80), channel_id=1, source_target_pairs={{0,1},{1,0},{2,3},{3,2},{4,5},{5,4},{6,7},{7,6},{8,9},{9,8},{10,11... | collective-permute-start | bytes 1972232 | tf_op jit(solution)/shard_map/ppermute | solution.py:527
  72.7 9.6 %collective-permute-done.8.refs_5_ = bf16[1024,256]{1,0:T(8,128)(2,1)S(1)} collective-permute-done((bf16[1024,256]{1,0:T(8,128)(2,1)S(1)}, bf16[1024,256]{1,0:T(8,128)(2,1)S(1)}, u32[]{:S(2)}, u32[]{:S(2)}) %collective-permute-start.8) | collective-permute-done | bytes 524320 | tf_op jit(solution)/shard_map/ppermute | solution.py:521
  82.3 2.8 %tower_backward.3 = (bf16[2560,128]{1,0:T(8,128)(2,1)S(1)}, bf16[2560,128]{1,0:T(8,128)(2,1)S(1)}) custom-call(bf16[1024,1024]{1,0:T(8,128)(2,1)S(1)} %copy-done, bf16[512,256]{1,0:T(8,128)(2,1)S(1)} %copy-done.5, bf16[1024,512]{1,0:T(8,128)(2,1)S(1)} %copy-done.2, f32[1024,256]{1,0:T(8,128)S(1)} %copy-done.3, f32[1024,256]{1,0:T(8,128)S(1)} %get-tuple-element.83.refs_4_, ...), custom_call_target="tpu_custom_call" | custom-call | flops 1610612736 | bytes 6815744 | tf_op jit(solution)/shard_map/tower_backward/pallas_call | solution.py:384
  85.1 3.9 %collective-permute-start.11 = (bf16[2560,128]{1,0:T(8,128)(2,1)S(1)}, bf16[2560,128]{1,0:T(8,128)(2,1)S(1)}, u32[]{:S(2)}, u32[]{:S(2)}) collective-permute-start(bf16[2560,128]{1,0:T(8,128)(2,1)S(1)} %get-tuple-element.88), channel_id=1, source_target_pairs={{0,1},{1,0},{2,3},{3,2},{4,5},{5,4},{6,7},{7,6},{8,9},{9,8},{10,11... | collective-permute-start | bytes 1966088 | tf_op jit(solution)/shard_map/ppermute | solution.py:527
  89.0 1.7 %collective-permute-done.11.got_items = bf16[2560,128]{1,0:T(8,128)(2,1)S(1)} collective-permute-done((bf16[2560,128]{1,0:T(8,128)(2,1)S(1)}, bf16[2560,128]{1,0:T(8,128)(2,1)S(1)}, u32[]{:S(2)}, u32[]{:S(2)}) %collective-permute-start.11) | collective-permute-done | bytes 655392 | tf_op jit(solution)/shard_map/ppermute | solution.py:527
  91.5 28.8 %all_to_all.10.parts = bf16[64,88,128]{2,1,0:T(8,128)(2,1)S(1)} all-to-all(bf16[64,88,128]{2,1,0:T(8,128)(2,1)S(1)} %pair.1), channel_id=1, replica_groups=mesh['row'=8,'chip'=8,'core'=2] {'row','chip'}, dimensions={0} | all-to-all | bytes 2883584 | tf_op jit(solution)/shard_map/all_to_all | solution.py:485
  121.1 24.8 %all_to_all.11.refs_0_ = bf16[64,80,128]{2,1,0:T(8,128)(2,1)S(1)} all-to-all(bf16[64,80,128]{2,1,0:T(8,128)(2,1)S(1)} %get-tuple-element.90), channel_id=1, replica_groups=mesh['row'=8,'chip'=8,'core'=2] {'row','chip'}, dimensions={0} | all-to-all | bytes 2621440 | tf_op jit(solution)/shard_map/all_to_all | solution.py:497
  145.9 2.5 %collective-permute-start.12 = (bf16[64,80,128]{2,1,0:T(8,128)(2,1)S(1)}, bf16[64,80,128]{2,1,0:T(8,128)(2,1)S(1)}, u32[]{:S(2)}, u32[]{:S(2)}) collective-permute-start(bf16[64,80,128]{2,1,0:T(8,128)(2,1)S(1)} %all_to_all.11.refs_0_), channel_id=1, source_target_pairs={{0,1},{1,0},{2,3},{3,2},{4,5},{5,4},{6,7},{7,6},{8,9},{9,8},{10,11... | collective-permute-start | bytes 3932168 | tf_op jit(solution)/shard_map/ppermute | solution.py:527
  148.5 1.6 %unpack.2 = (f32[1024,512]{1,0:T(8,128)}, f32[512,256]{1,0:T(8,128)}, f32[1024,512]{1,0:T(8,128)}, f32[512,256]{1,0:T(8,128)}) custom-call(bf16[64,80,128]{2,1,0:T(8,128)(2,1)S(1)} %all_to_all.11.refs_0_), custom_call_target="tpu_custom_call" | custom-call | flops 100000000 | bytes 1966080 | tf_op jit(solution)/shard_map/unpack/pallas_call | solution.py:455
  151.1 1.6 %unpack.3 = (f32[1024,512]{1,0:T(8,128)}, f32[512,256]{1,0:T(8,128)}, f32[1024,512]{1,0:T(8,128)}, f32[512,256]{1,0:T(8,128)}) custom-call(bf16[64,80,128]{2,1,0:T(8,128)(2,1)S(1)} %collective-permute-done.12.refs_0_, f32[1024,512]{1,0:T(8,128)} %get-tuple-element.91.refs_1_, ...), custom_call_target="tpu_custom_call", output_to_operand_aliasing={{0}: (1, {}), {1}: (2, {}), {2}: (3, {}), {3}: (4, {})} | custom-call | flops 100000000 | bytes 1966080 | tf_op jit(solution)/shard_map/unpack/pallas_call | solution.py:455
  (39 shorter events, 12.9 us)
Async XLA Ops:
  0.6 10.2 %copy-start.1 = (bf16[1024,1024]{1,0:T(8,128)(2,1)S(1)}, bf16[1024,1024]{1,0:T(8,128)(2,1)}, u32[]{:S(2)}) copy-start(bf16[1024,1024]{1,0:T(8,128)(2,1)} %refs_0_.4) | copy-start | bytes 6291460
  0.6 10.2 %copy-start.6 = (bf16[512,256]{1,0:T(8,128)(2,1)S(1)}, bf16[512,256]{1,0:T(8,128)(2,1)}, u32[]{:S(2)}) copy-start(bf16[512,256]{1,0:T(8,128)(2,1)} %refs_1_.4) | copy-start | bytes 786436
  0.7 10.2 %copy-start.8 = (bf16[1024,512]{1,0:T(8,128)(2,1)S(1)}, bf16[1024,512]{1,0:T(8,128)(2,1)}, u32[]{:S(2)}) copy-start(bf16[1024,512]{1,0:T(8,128)(2,1)} %first.1) | copy-start | bytes 3145732
  6.2 9.7 %copy-start.4 = (bf16[1024,256]{1,0:T(8,128)(2,1)S(1)}, bf16[1024,256]{1,0:T(8,128)(2,1)}, u32[]{:S(2)}) copy-start(bf16[1024,256]{1,0:T(8,128)(2,1)} %get-tuple-element.54.refs_0_.refs_2_) | copy-start | bytes 1572868
  6.2 11.0 %copy-start.7 = (f32[2,1024]{1,0:T(2,128)S(1)}, f32[2,1024]{1,0:T(2,128)}, u32[]{:S(2)}) copy-start(f32[2,1024]{1,0:T(2,128)} %get-tuple-element.56.refs_2_.refs_3_.refs_5_.refs_4_) | copy-start | bytes 24580
  6.2 26.7 %collective-permute-start.4 = (bf16[1024,256]{1,0:T(8,128)(2,1)}, bf16[1024,256]{1,0:T(8,128)(2,1)S(1)}, u32[]{:S(2)}, u32[]{:S(2)}) collective-permute-start(bf16[1024,256]{1,0:T(8,128)(2,1)} %get-tuple-element.54.refs_0_.refs_2_), channel_id=1, source_target_pairs={{0,48},{16,0},{32,16},{48,32},{64,112},{80,64},{96,80},{112,96},{1... | collective-permute-start | bytes 1572872 | tf_op jit(solution)/shard_map/ppermute | solution.py:521
  10.8 22.0 %collective-permute-start.3 = (bf16[1024,256]{1,0:T(8,128)(2,1)}, bf16[1024,256]{1,0:T(8,128)(2,1)S(1)}, u32[]{:S(2)}, u32[]{:S(2)}) collective-permute-start(bf16[1024,256]{1,0:T(8,128)(2,1)} %get-tuple-element.54.refs_0_.refs_2_), channel_id=1, source_target_pairs={{0,16},{16,32},{32,48},{48,0},{64,80},{80,96},{96,112},{112,64},{1... | collective-permute-start | bytes 1572872 | tf_op jit(solution)/shard_map/ppermute | solution.py:521
  13.1 22.3 %collective-permute-start.1 = (bf16[1024,256]{1,0:T(8,128)(2,1)S(1)}, bf16[1024,256]{1,0:T(8,128)(2,1)S(1)}, u32[]{:S(2)}, u32[]{:S(2)}) collective-permute-start(bf16[1024,256]{1,0:T(8,128)(2,1)S(1)} %get-tuple-element.55.refs_1_.refs_2_.refs_3_), channel_id=1, source_target_pairs={{0,64},{16,80},{32,96},{48,112},{64,0},{80,16},{96,32},{112,48},{1... | collective-permute-start | bytes 1572872 | tf_op jit(solution)/shard_map/ppermute | solution.py:524
  15.9 23.0 %collective-permute-start = (bf16[1024,256]{1,0:T(8,128)(2,1)S(1)}, bf16[1024,256]{1,0:T(8,128)(2,1)S(1)}, u32[]{:S(2)}, u32[]{:S(2)}) collective-permute-start(bf16[1024,256]{1,0:T(8,128)(2,1)S(1)} %copy-done.4), channel_id=1, source_target_pairs={{0,32},{16,48},{32,0},{48,16},{64,96},{80,112},{96,64},{112,80},{1... | collective-permute-start | bytes 1572872 | tf_op jit(solution)/shard_map/ppermute | solution.py:521
  17.2 18.1 %collective-permute-start.2 = (f32[2,1024]{1,0:T(2,128)S(1)}, f32[2,1024]{1,0:T(2,128)S(1)}, u32[]{:S(2)}, u32[]{:S(2)}) collective-permute-start(f32[2,1024]{1,0:T(2,128)S(1)} %copy-done.7), channel_id=1, source_target_pairs={{0,64},{16,80},{32,96},{48,112},{64,0},{80,16},{96,32},{112,48},{1... | collective-permute-start | bytes 24584 | tf_op jit(solution)/shard_map/ppermute | solution.py:524
  41.4 4.4 %collective-permute-start.5 = (f32[4,1024]{1,0:T(4,128)S(1)}, f32[4,1024]{1,0:T(4,128)S(1)}, u32[]{:S(2)}, u32[]{:S(2)}) collective-permute-start(f32[4,1024]{1,0:T(4,128)S(1)} %get-tuple-element.60.refs_0_), channel_id=1, source_target_pairs={{0,64},{16,80},{32,96},{48,112},{64,0},{80,16},{96,32},{112,48},{1... | collective-permute-start | bytes 49160 | tf_op jit(solution)/shard_map/ppermute | solution.py:524
  51.8 11.6 %collective-permute-start.6 = (bf16[256,1024]{1,0:T(8,128)(2,1)S(1)}, bf16[256,1024]{1,0:T(8,128)(2,1)S(1)}, u32[]{:S(2)}, u32[]{:S(2)}) collective-permute-start(bf16[256,1024]{1,0:T(8,128)(2,1)S(1)} %get-tuple-element.77), channel_id=1, source_target_pairs={{0,64},{16,80},{32,96},{48,112},{64,0},{80,16},{96,32},{112,48},{1... | collective-permute-start | bytes 1572872 | tf_op jit(solution)/shard_map/ppermute | solution.py:524
  57.3 14.7 %collective-permute-start.10 = (bf16[1024,256]{1,0:T(8,128)(2,1)S(1)}, bf16[1024,256]{1,0:T(8,128)(2,1)S(1)}, u32[]{:S(2)}, u32[]{:S(2)}) collective-permute-start(bf16[1024,256]{1,0:T(8,128)(2,1)S(1)} %get-tuple-element.86), channel_id=1, source_target_pairs={{0,16},{16,32},{32,48},{48,0},{64,80},{80,96},{96,112},{112,64},{1... | collective-permute-start | bytes 1572872 | tf_op jit(solution)/shard_map/ppermute | solution.py:521
  57.4 15.3 %collective-permute-start.9 = (bf16[1024,256]{1,0:T(8,128)(2,1)S(1)}, bf16[1024,256]{1,0:T(8,128)(2,1)S(1)}, u32[]{:S(2)}, u32[]{:S(2)}) collective-permute-start(bf16[1024,256]{1,0:T(8,128)(2,1)S(1)} %get-tuple-element.85), channel_id=1, source_target_pairs={{0,48},{16,0},{32,16},{48,32},{64,112},{80,64},{96,80},{112,96},{1... | collective-permute-start | bytes 1572872 | tf_op jit(solution)/shard_map/ppermute | solution.py:521
  60.9 21.4 %collective-permute-start.8 = (bf16[1024,256]{1,0:T(8,128)(2,1)S(1)}, bf16[1024,256]{1,0:T(8,128)(2,1)S(1)}, u32[]{:S(2)}, u32[]{:S(2)}) collective-permute-start(bf16[1024,256]{1,0:T(8,128)(2,1)S(1)} %get-tuple-element.84), channel_id=1, source_target_pairs={{0,32},{16,48},{32,0},{48,16},{64,96},{80,112},{96,64},{112,80},{1... | collective-permute-start | bytes 1572872 | tf_op jit(solution)/shard_map/ppermute | solution.py:521
  63.3 18.9 %copy-start = (bf16[1024,1024]{1,0:T(8,128)(2,1)S(1)}, bf16[1024,1024]{1,0:T(8,128)(2,1)}, u32[]{:S(2)}) copy-start(bf16[1024,1024]{1,0:T(8,128)(2,1)} %refs_0_.5) | copy-start | bytes 6291460
  63.4 18.9 %copy-start.2 = (bf16[1024,512]{1,0:T(8,128)(2,1)S(1)}, bf16[1024,512]{1,0:T(8,128)(2,1)}, u32[]{:S(2)}) copy-start(bf16[1024,512]{1,0:T(8,128)(2,1)} %get-tuple-element.81.refs_2_) | copy-start | bytes 3145732
  63.4 18.9 %copy-start.3 = (f32[1024,256]{1,0:T(8,128)S(1)}, f32[1024,256]{1,0:T(8,128)}, u32[]{:S(2)}) copy-start(f32[1024,256]{1,0:T(8,128)} %get-tuple-element.82.refs_3_) | copy-start | bytes 3145732
  63.4 18.9 %copy-start.5 = (bf16[512,256]{1,0:T(8,128)(2,1)S(1)}, bf16[512,256]{1,0:T(8,128)(2,1)}, u32[]{:S(2)}) copy-start(bf16[512,256]{1,0:T(8,128)(2,1)} %refs_1_.5) | copy-start | bytes 786436
  66.6 24.2 %collective-permute-start.7 = (bf16[2568,128]{1,0:T(8,128)(2,1)S(1)}, bf16[2568,128]{1,0:T(8,128)(2,1)S(1)}, u32[]{:S(2)}, u32[]{:S(2)}) collective-permute-start(bf16[2568,128]{1,0:T(8,128)(2,1)S(1)} %get-tuple-element.80), channel_id=1, source_target_pairs={{0,1},{1,0},{2,3},{3,2},{4,5},{5,4},{6,7},{7,6},{8,9},{9,8},{10,11... | collective-permute-start | bytes 1972232 | tf_op jit(solution)/shard_map/ppermute | solution.py:527
  85.1 5.6 %collective-permute-start.11 = (bf16[2560,128]{1,0:T(8,128)(2,1)S(1)}, bf16[2560,128]{1,0:T(8,128)(2,1)S(1)}, u32[]{:S(2)}, u32[]{:S(2)}) collective-permute-start(bf16[2560,128]{1,0:T(8,128)(2,1)S(1)} %get-tuple-element.88), channel_id=1, source_target_pairs={{0,1},{1,0},{2,3},{3,2},{4,5},{5,4},{6,7},{7,6},{8,9},{9,8},{10,11... | collective-permute-start | bytes 1966088 | tf_op jit(solution)/shard_map/ppermute | solution.py:527
  145.9 5.2 %collective-permute-start.12 = (bf16[64,80,128]{2,1,0:T(8,128)(2,1)S(1)}, bf16[64,80,128]{2,1,0:T(8,128)(2,1)S(1)}, u32[]{:S(2)}, u32[]{:S(2)}) collective-permute-start(bf16[64,80,128]{2,1,0:T(8,128)(2,1)S(1)} %all_to_all.11.refs_0_), channel_id=1, source_target_pairs={{0,1},{1,0},{2,3},{3,2},{4,5},{5,4},{6,7},{7,6},{8,9},{9,8},{10,11... | collective-permute-start | bytes 3932168 | tf_op jit(solution)/shard_map/ppermute | solution.py:527

commit v2 on v1

--- a/solution.py
+++ b/solution.py
@@ -155,6 +155,11 @@
     users, metas, refs = refs[:n_users], refs[n_users : 2 * n_users], refs[2 * n_users :]
     before, refs = refs[:n_sums], refs[n_sums:]
     exps, after = refs[: len(blocks)], refs[len(blocks) :]
+    if last:
+        joined, half = after[1], items[0].shape[0]
+        for k in range(2):
+            joined[k * half : (k + 1) * half, :] = items[k][...]
+        items = (joined,)
     for side in range(n_users):
         n, emb = users[side].shape
         u = users[side][...]
@@ -189,10 +194,10 @@
 
 def scores(blocks, items, users, metas, sums, last=False):
     n, emb = users[0].shape
-    m = items[0].shape[0]
+    m = items[0].shape[0] * (2 if last else 1)
     results = [jax.ShapeDtypeStruct((m, n), BF)] * len(blocks)
     if last:
-        results += [jax.ShapeDtypeStruct((4, n), F32)]
+        results += [jax.ShapeDtypeStruct((4, n), F32), jax.ShapeDtypeStruct((m, emb), BF)]
     else:
         results += [jax.ShapeDtypeStruct((2, n), F32)] * len(users)
     operands = (*items, *users, *metas, *sums)
@@ -207,6 +212,25 @@
         name="scores",
     )(*operands)
     return out[:count], out[count:]
+
+
+def halves_kernel(a, b, low, high):
+    half = low.shape[0]
+    low[...] = a[0:half, :]
+    high[...] = b[half : 2 * half, :]
+
+
+def first_and_second_half(a, b):
+    shape = jax.ShapeDtypeStruct((a.shape[0] // 2, a.shape[1]), a.dtype)
+    return pl.pallas_call(
+        halves_kernel,
+        in_specs=in_vmem(2),
+        out_specs=in_vmem(2),
+        out_shape=[shape, shape],
+        cost_estimate=cost(10**6, 4 * a.size),
+        compiler_params=grant(4),
+        name="halves",
+    )(a, b)
 
 
 def three_terms(value):
@@ -535,24 +559,28 @@
     )
     metas = (meta, partner(meta))
     items = [item_vec]
-    for slot in range(1, NZ):
+    for slot in (1, 2):
         items.append(along_z(item_vec, HOPS[slot]))
     user_vec, user_hidden, user_out = tower_forward(
         customer_inputs, customer_initial_weights, customer_final_weights
     )
     users = (user_vec, partner(user_vec))
+    far = []
+    for slot, half in zip((1, 2), first_and_second_half(items[1], items[2])):
+        far.append(along_z(half, HOPS[slot]))
 
     exps = [[None] * NZ, [None] * NZ]
     (exps[0][0],), (own_sums,) = scores(((0, 0, 0),), items[:1], users[:1], metas[:1], ())
     exps[0][1:3], (own_sums,) = scores(
-        ((0, 1, 0), (1, 2, 0)), items[1:3], users[:1], metas[:1], (own_sums,)
+        ((0, 1, 0), (1, 2, 0)), items[1:], users[:1], metas[:1], (own_sums,)
     )
     exps[1][0:3], (other_sums,) = scores(
-        ((0, 0, 0), (1, 1, 0), (2, 2, 0)), items[:3], users[1:], metas[1:], ()
-    )
-    (exps[0][3], exps[1][3]), (mine,) = scores(
-        ((0, 3, 0), (0, 3, 1)), items[3:], users, metas, (own_sums, other_sums), last=True
-    )
+        ((0, 0, 0), (1, 1, 0), (2, 2, 0)), items, users[1:], metas[1:], ()
+    )
+    (exps[0][3], exps[1][3]), (mine, far) = scores(
+        ((0, 3, 0), (0, 3, 1)), far, users, metas, (own_sums, other_sums), last=True
+    )
+    items.append(far)
     theirs = partner(mine)
 
     unit = 1.0 / (emb * m)

time: 153 us -> 149 us (0.974)
  waiting for transfers between devices: 28.6 us -> 21.8 us
    ppermute x6 -> x7, waiting for transfers between devices: 24.4 us -> 15.7 us  [along_z(): return lax.ppermute(value, 'row', pairs)]
    ppermute x4, waiting for transfers between devices: 1.36 us -> 3.3 us  [partner(): lax.ppermute(value, 'row', [(k, (k + NZ) % n_row) for k in range(n_row)])]
    ppermute x6 -> x7, starting transfers between devices: 10.6 us -> 10.1 us  [along_z(): return lax.ppermute(value, 'row', pairs)]
  transfers between devices with their start and end apart: 13 -> 14, of which waited for: 6 -> 7; matrix products, arithmetic and copies ran while one was open for 0% -> 0% of each run, Pallas kernels for 14% -> 14%
where the time goes in v2:
time: 149 us; the launch traced here: 148 us
  blocking collectives  54.7 us (37%)
  Pallas kernels  38.6 us (26%)
  starting transfers between devices  32.2 us (22%)
  waiting for transfers between devices  21.8 us (15%)
    all_to_all x1, blocking collectives, sum_over_all(): parts = lax.all_to_all(to_sum, peers, 0, 0, tiled=True)  29.9 us
    all_to_all x1, blocking collectives, sum_over_all(): mine = lax.all_to_all(to_share, peers, 0, 0, tiled=True)  24.8 us
    ppermute x7, waiting for transfers between devices, along_z(): return lax.ppermute(value, 'row', pairs)  15.7 us
    ppermute x3, starting transfers between devices, other_core(): return lax.ppermute(value, 'core', [(0, 1), (1, 0)])  13.2 us
    ppermute x7, starting transfers between devices, along_z(): return lax.ppermute(value, 'row', pairs)  10.1 us
    pallas_call x5, Pallas kernels, vector_grads(): pl.pallas_call(functools.partial(vectors_kernel, plan, unit), in_specs=in...  10.1 us
    pallas_call x4, Pallas kernels, scores(): pl.pallas_call(functools.partial(scores_kernel, blocks, len(items), len(u...  10 us
    ppermute x4, starting transfers between devices, partner(): lax.ppermute(value, 'row', [(k, (k + NZ) % n_row) for k in range(n_row)])  8.91 us
  transfers between devices with their start and end apart: 14, of which 7 were waited for; matrix products, arithmetic and copies ran while one was open for 0% of the time, Pallas kernels for 14%

profile of v2, /device:TPU:1, one launch (start us, length us, event | category | flops | bytes accessed | tf_op | source)
XLA Modules:
  0.0 148.4 jit_solution(7172402412691846602)
XLA Ops:
  0.7 5.5 %tower_forward.3 = (bf16[1024,256]{1,0:T(8,128)(2,1)}, bf16[1024,512]{1,0:T(8,128)(2,1)}, f32[1024,256]{1,0:T(8,128)}, f32[2,1024]{1,0:T(2,128)}) custom-call(bf16[1024,1024]{1,0:T(8,128)(2,1)} %refs_0_.5, bf16[1024,512]{1,0:T(8,128)(2,1)} %refs_1_.3, bf16[512,256]{1,0:T(8,128)(2,1)} %refs_1_.5, bf16[8,128]{1,0:T(8,128)(2,1)} %bitcast.4, s32[8,128]{1,0:T(8,128)} %bitcast.3), custom_call_target="tpu_custom_call" | custom-call | flops 1342177280 | bytes 4718592 | tf_op jit(solution)/shard_map/tower_forward/pallas_call | solution.py:129
  6.2 4.6 %collective-permute-start.1 = (bf16[1024,256]{1,0:T(8,128)(2,1)}, bf16[1024,256]{1,0:T(8,128)(2,1)S(1)}, u32[]{:S(2)}, u32[]{:S(2)}) collective-permute-start(bf16[1024,256]{1,0:T(8,128)(2,1)} %get-tuple-element.57.refs_0_.refs_2_), channel_id=1, source_target_pairs={{0,48},{16,0},{32,16},{48,32},{64,112},{80,64},{96,80},{112,96},{1... | collective-permute-start | bytes 1572872 | tf_op jit(solution)/shard_map/ppermute | solution.py:545
  10.9 2.2 %tower_forward.2 = (bf16[1024,256]{1,0:T(8,128)(2,1)S(1)}, bf16[1024,512]{1,0:T(8,128)(2,1)S(1)}, f32[1024,256]{1,0:T(8,128)S(1)}) custom-call(bf16[1024,1024]{1,0:T(8,128)(2,1)S(1)} %copy-done.1, bf16[1024,512]{1,0:T(8,128)(2,1)S(1)} %copy-done.8, bf16[512,256]{1,0:T(8,128)(2,1)S(1)} %copy-done.6), custom_call_target="tpu_custom_call" | custom-call | flops 1342177280 | bytes 4718592 | tf_op jit(solution)/shard_map/tower_forward/pallas_call | solution.py:69
  13.1 2.8 %collective-permute-start.4 = (bf16[1024,256]{1,0:T(8,128)(2,1)S(1)}, bf16[1024,256]{1,0:T(8,128)(2,1)S(1)}, u32[]{:S(2)}, u32[]{:S(2)}) collective-permute-start(bf16[1024,256]{1,0:T(8,128)(2,1)S(1)} %get-tuple-element.60.refs_1_.refs_2_.refs_3_), channel_id=1, source_target_pairs={{0,64},{16,80},{32,96},{48,112},{64,0},{80,16},{96,32},{112,48},{1... | collective-permute-start | bytes 1572872 | tf_op jit(solution)/shard_map/ppermute | solution.py:548
  16.1 5.6 %collective-permute-done.1.b.refs_1_.refs_2_.refs_4_ = bf16[1024,256]{1,0:T(8,128)(2,1)S(1)} collective-permute-done((bf16[1024,256]{1,0:T(8,128)(2,1)}, bf16[1024,256]{1,0:T(8,128)(2,1)S(1)}, u32[]{:S(2)}, u32[]{:S(2)}) %collective-permute-start.1) | collective-permute-done | bytes 524320 | tf_op jit(solution)/shard_map/ppermute | solution.py:545
  21.8 3.0 %collective-permute-done.a.refs_0_.refs_1_.refs_3_.refs_2_ = bf16[1024,256]{1,0:T(8,128)(2,1)S(1)} collective-permute-done((bf16[1024,256]{1,0:T(8,128)(2,1)}, bf16[1024,256]{1,0:T(8,128)(2,1)S(1)}, u32[]{:S(2)}, u32[]{:S(2)}) %collective-permute-start) | collective-permute-done | bytes 524320 | tf_op jit(solution)/shard_map/ppermute | solution.py:545
  24.9 2.7 %collective-permute-start.3 = (bf16[512,256]{1,0:T(8,128)(2,1)S(1)}, bf16[512,256]{1,0:T(8,128)(2,1)S(1)}, u32[]{:S(2)}, u32[]{:S(2)}) collective-permute-start(bf16[512,256]{1,0:T(8,128)(2,1)S(1)} %get-tuple-element.59), channel_id=1, source_target_pairs={{0,48},{16,0},{32,16},{48,32},{64,112},{80,64},{96,80},{112,96},{1... | collective-permute-start | bytes 786440 | tf_op jit(solution)/shard_map/ppermute | solution.py:545
  28.9 2.5 %scores.5 = (bf16[1024,1024]{1,0:T(8,128)(2,1)S(1)}, bf16[1024,1024]{1,0:T(8,128)(2,1)S(1)}, f32[2,1024]{1,0:T(2,128)S(1)}) custom-call(bf16[1024,256]{1,0:T(8,128)(2,1)S(1)} %collective-permute-done.a.refs_0_.refs_1_.refs_3_.refs_2_, bf16[1024,256]{1,0:T(8,128)(2,1)S(1)} %collective-permute-done.1.b.refs_1_.refs_2_.refs_4_, ...), custom_call_target="tpu_custom_call" | custom-call | flops 1073741824 | bytes 4194304 | tf_op jit(solution)/shard_map/scores/pallas_call | solution.py:205
  31.4 3.7 %scores.6 = (bf16[1024,1024]{1,0:T(8,128)(2,1)S(1)}, bf16[1024,1024]{1,0:T(8,128)(2,1)S(1)}, bf16[1024,1024]{1,0:T(8,128)(2,1)S(1)}, f32[2,1024]{1,0:T(2,128)S(1)}) custom-call(bf16[1024,256]{1,0:T(8,128)(2,1)S(1)} %copy-done.4, bf16[1024,256]{1,0:T(8,128)(2,1)S(1)} %collective-permute-done.a.refs_0_.refs_1_.refs_3_.refs_2_, ...), custom_call_target="tpu_custom_call" | custom-call | flops 1610612736 | bytes 6291456 | tf_op jit(solution)/shard_map/scores/pallas_call | solution.py:205
  35.1 2.5 %scores.7 = (bf16[1024,1024]{1,0:T(8,128)(2,1)S(1)}, bf16[1024,1024]{1,0:T(8,128)(2,1)S(1)}, f32[4,1024]{1,0:T(4,128)S(1)}, bf16[1024,256]{1,0:T(8,128)(2,1)S(1)}) custom-call(bf16[512,256]{1,0:T(8,128)(2,1)S(1)} %collective-permute-done.2.refs_0_, bf16[512,256]{1,0:T(8,128)(2,1)S(1)} %collective-permute-done.3.refs_1_, ...), custom_call_target="tpu_custom_call" | custom-call | flops 1073741824 | bytes 4194304 | tf_op jit(solution)/shard_map/scores/pallas_call | solution.py:205
  37.6 3.0 %collective-permute-start.6 = (f32[4,1024]{1,0:T(4,128)S(1)}, f32[4,1024]{1,0:T(4,128)S(1)}, u32[]{:S(2)}, u32[]{:S(2)}) collective-permute-start(f32[4,1024]{1,0:T(4,128)S(1)} %get-tuple-element.65.refs_0_), channel_id=1, source_target_pairs={{0,64},{16,80},{32,96},{48,112},{64,0},{80,16},{96,32},{112,48},{1... | collective-permute-start | bytes 49160 | tf_op jit(solution)/shard_map/ppermute | solution.py:548
  42.0 2.5 %vector_grads.5 = (bf16[1024,256]{1,0:T(8,128)(2,1)S(1)}, f32[256,1024]{1,0:T(8,128)S(1)}, f32[256,1024]{1,0:T(8,128)S(1)}) custom-call(f32[4,1024]{1,0:T(4,128)S(1)} %get-tuple-element.65.refs_0_, f32[4,1024]{1,0:T(4,128)S(1)} %collective-permute-done.6.refs_1_, bf16[1024,256]{1,0:T(8,128)(2,1)S(1)} %get-tuple-element.70.refs_2_, ...), custom_call_target="tpu_custom_call" | custom-call | flops 2147483648 | bytes 6815744 | tf_op jit(solution)/shard_map/vector_grads/pallas_call | solution.py:334
  44.5 3.6 %vector_grads.6 = (f32[1024,256]{1,0:T(8,128)S(1)}, f32[1024,256]{1,0:T(8,128)S(1)}, f32[1024,256]{1,0:T(8,128)S(1)}, bf16[256,1024]{1,0:T(8,128)(2,1)S(1)}) custom-call(f32[4,1024]{1,0:T(4,128)S(1)} %get-tuple-element.65.refs_0_, f32[4,1024]{1,0:T(4,128)S(1)} %collective-permute-done.6.refs_1_, bf16[1024,256]{1,0:T(8,128)(2,1)S(1)} %copy-done.4, ...), custom_call_target="tpu_custom_call" | custom-call | flops 3221225472 | bytes 8912896 | tf_op jit(solution)/shard_map/vector_grads/pallas_call | solution.py:334
  48.1 2.8 %collective-permute-start.7 = (bf16[256,1024]{1,0:T(8,128)(2,1)S(1)}, bf16[256,1024]{1,0:T(8,128)(2,1)S(1)}, u32[]{:S(2)}, u32[]{:S(2)}) collective-permute-start(bf16[256,1024]{1,0:T(8,128)(2,1)S(1)} %get-tuple-element.83), channel_id=1, source_target_pairs={{0,64},{16,80},{32,96},{48,112},{64,0},{80,16},{96,32},{112,48},{1... | collective-permute-start | bytes 1572872 | tf_op jit(solution)/shard_map/ppermute | solution.py:548
  53.7 2.7 %collective-permute-start.10 = (bf16[1024,256]{1,0:T(8,128)(2,1)S(1)}, bf16[1024,256]{1,0:T(8,128)(2,1)S(1)}, u32[]{:S(2)}, u32[]{:S(2)}) collective-permute-start(bf16[1024,256]{1,0:T(8,128)(2,1)S(1)} %get-tuple-element.91), channel_id=1, source_target_pairs={{0,48},{16,0},{32,16},{48,32},{64,112},{80,64},{96,80},{112,96},{1... | collective-permute-start | bytes 1572872 | tf_op jit(solution)/shard_map/ppermute | solution.py:545
  57.7 1.9 %collective-permute-done.7.refs_5_ = bf16[256,1024]{1,0:T(8,128)(2,1)S(1)} collective-permute-done((bf16[256,1024]{1,0:T(8,128)(2,1)S(1)}, bf16[256,1024]{1,0:T(8,128)(2,1)S(1)}, u32[]{:S(2)}, u32[]{:S(2)}) %collective-permute-start.7) | collective-permute-done | bytes 524320 | tf_op jit(solution)/shard_map/ppermute | solution.py:548
  59.7 3.2 %tower_backward.2 = (bf16[2560,128]{1,0:T(8,128)(2,1)S(1)}, bf16[2568,128]{1,0:T(8,128)(2,1)S(1)}) custom-call(bf16[1024,1024]{1,0:T(8,128)(2,1)S(1)} %copy-done.1, bf16[512,256]{1,0:T(8,128)(2,1)S(1)} %copy-done.6, bf16[1024,512]{1,0:T(8,128)(2,1)S(1)} %get-tuple-element.55.refs_2_, f32[1024,256]{1,0:T(8,128)S(1)} %get-tuple-element.56.refs_3_, ...), custom_call_target="tpu_custom_call" | custom-call | flops 1610612736 | bytes 6815744 | tf_op jit(solution)/shard_map/tower_backward/pallas_call | solution.py:408
  62.8 4.5 %collective-permute-start.8 = (bf16[2568,128]{1,0:T(8,128)(2,1)S(1)}, bf16[2568,128]{1,0:T(8,128)(2,1)S(1)}, u32[]{:S(2)}, u32[]{:S(2)}) collective-permute-start(bf16[2568,128]{1,0:T(8,128)(2,1)S(1)} %get-tuple-element.86), channel_id=1, source_target_pairs={{0,1},{1,0},{2,3},{3,2},{4,5},{5,4},{6,7},{7,6},{8,9},{9,8},{10,11... | collective-permute-start | bytes 1972232 | tf_op jit(solution)/shard_map/ppermute | solution.py:551
  67.3 7.0 %collective-permute-done.9.refs_5_ = bf16[1024,256]{1,0:T(8,128)(2,1)S(1)} collective-permute-done((bf16[1024,256]{1,0:T(8,128)(2,1)S(1)}, bf16[1024,256]{1,0:T(8,128)(2,1)S(1)}, u32[]{:S(2)}, u32[]{:S(2)}) %collective-permute-start.9) | collective-permute-done | bytes 524320 | tf_op jit(solution)/shard_map/ppermute | solution.py:545
  74.4 2.8 %tower_backward.3 = (bf16[2560,128]{1,0:T(8,128)(2,1)S(1)}, bf16[2560,128]{1,0:T(8,128)(2,1)S(1)}) custom-call(bf16[1024,1024]{1,0:T(8,128)(2,1)S(1)} %copy-done, bf16[512,256]{1,0:T(8,128)(2,1)S(1)} %copy-done.5, bf16[1024,512]{1,0:T(8,128)(2,1)S(1)} %copy-done.2, f32[1024,256]{1,0:T(8,128)S(1)} %copy-done.3, f32[1024,256]{1,0:T(8,128)S(1)} %get-tuple-element.89.refs_4_, ...), custom_call_target="tpu_custom_call" | custom-call | flops 1610612736 | bytes 6815744 | tf_op jit(solution)/shard_map/tower_backward/pallas_call | solution.py:408
  77.2 6.2 %collective-permute-start.12 = (bf16[2560,128]{1,0:T(8,128)(2,1)S(1)}, bf16[2560,128]{1,0:T(8,128)(2,1)S(1)}, u32[]{:S(2)}, u32[]{:S(2)}) collective-permute-start(bf16[2560,128]{1,0:T(8,128)(2,1)S(1)} %get-tuple-element.94), channel_id=1, source_target_pairs={{0,1},{1,0},{2,3},{3,2},{4,5},{5,4},{6,7},{7,6},{8,9},{9,8},{10,11... | collective-permute-start | bytes 1966088 | tf_op jit(solution)/shard_map/ppermute | solution.py:551
  85.9 29.9 %all_to_all.10.parts = bf16[64,88,128]{2,1,0:T(8,128)(2,1)S(1)} all-to-all(bf16[64,88,128]{2,1,0:T(8,128)(2,1)S(1)} %pair.1), channel_id=1, replica_groups=mesh['row'=8,'chip'=8,'core'=2] {'row','chip'}, dimensions={0} | all-to-all | bytes 2883584 | tf_op jit(solution)/shard_map/all_to_all | solution.py:509
  116.6 24.8 %all_to_all.11.refs_0_ = bf16[64,80,128]{2,1,0:T(8,128)(2,1)S(1)} all-to-all(bf16[64,80,128]{2,1,0:T(8,128)(2,1)S(1)} %get-tuple-element.96), channel_id=1, replica_groups=mesh['row'=8,'chip'=8,'core'=2] {'row','chip'}, dimensions={0} | all-to-all | bytes 2621440 | tf_op jit(solution)/shard_map/all_to_all | solution.py:521
  141.4 2.5 %collective-permute-start.13 = (bf16[64,80,128]{2,1,0:T(8,128)(2,1)S(1)}, bf16[64,80,128]{2,1,0:T(8,128)(2,1)S(1)}, u32[]{:S(2)}, u32[]{:S(2)}) collective-permute-start(bf16[64,80,128]{2,1,0:T(8,128)(2,1)S(1)} %all_to_all.11.refs_0_), channel_id=1, source_target_pairs={{0,1},{1,0},{2,3},{3,2},{4,5},{5,4},{6,7},{7,6},{8,9},{9,8},{10,11... | collective-permute-start | bytes 3932168 | tf_op jit(solution)/shard_map/ppermute | solution.py:551
  (42 shorter events, 14.7 us)
Async XLA Ops:
  0.6 10.2 %copy-start.1 = (bf16[1024,1024]{1,0:T(8,128)(2,1)S(1)}, bf16[1024,1024]{1,0:T(8,128)(2,1)}, u32[]{:S(2)}) copy-start(bf16[1024,1024]{1,0:T(8,128)(2,1)} %refs_0_.4) | copy-start | bytes 6291460
  0.6 10.2 %copy-start.6 = (bf16[512,256]{1,0:T(8,128)(2,1)S(1)}, bf16[512,256]{1,0:T(8,128)(2,1)}, u32[]{:S(2)}) copy-start(bf16[512,256]{1,0:T(8,128)(2,1)} %refs_1_.4) | copy-start | bytes 786436
  0.7 10.2 %copy-start.8 = (bf16[1024,512]{1,0:T(8,128)(2,1)S(1)}, bf16[1024,512]{1,0:T(8,128)(2,1)}, u32[]{:S(2)}) copy-start(bf16[1024,512]{1,0:T(8,128)(2,1)} %first.1) | copy-start | bytes 3145732
  6.2 9.7 %copy-start.7 = (f32[2,1024]{1,0:T(2,128)S(1)}, f32[2,1024]{1,0:T(2,128)}, u32[]{:S(2)}) copy-start(f32[2,1024]{1,0:T(2,128)} %get-tuple-element.61.refs_2_.refs_3_.refs_4_.refs_5_) | copy-start | bytes 24580
  6.2 21.4 %copy-start.4 = (bf16[1024,256]{1,0:T(8,128)(2,1)S(1)}, bf16[1024,256]{1,0:T(8,128)(2,1)}, u32[]{:S(2)}) copy-start(bf16[1024,256]{1,0:T(8,128)(2,1)} %get-tuple-element.57.refs_0_.refs_2_) | copy-start | bytes 1572868
  6.2 15.6 %collective-permute-start.1 = (bf16[1024,256]{1,0:T(8,128)(2,1)}, bf16[1024,256]{1,0:T(8,128)(2,1)S(1)}, u32[]{:S(2)}, u32[]{:S(2)}) collective-permute-start(bf16[1024,256]{1,0:T(8,128)(2,1)} %get-tuple-element.57.refs_0_.refs_2_), channel_id=1, source_target_pairs={{0,48},{16,0},{32,16},{48,32},{64,112},{80,64},{96,80},{112,96},{1... | collective-permute-start | bytes 1572872 | tf_op jit(solution)/shard_map/ppermute | solution.py:545
  10.8 13.9 %collective-permute-start = (bf16[1024,256]{1,0:T(8,128)(2,1)}, bf16[1024,256]{1,0:T(8,128)(2,1)S(1)}, u32[]{:S(2)}, u32[]{:S(2)}) collective-permute-start(bf16[1024,256]{1,0:T(8,128)(2,1)} %get-tuple-element.57.refs_0_.refs_2_), channel_id=1, source_target_pairs={{0,16},{16,32},{32,48},{48,0},{64,80},{80,96},{96,112},{112,64},{1... | collective-permute-start | bytes 1572872 | tf_op jit(solution)/shard_map/ppermute | solution.py:545
  13.1 18.3 %collective-permute-start.4 = (bf16[1024,256]{1,0:T(8,128)(2,1)S(1)}, bf16[1024,256]{1,0:T(8,128)(2,1)S(1)}, u32[]{:S(2)}, u32[]{:S(2)}) collective-permute-start(bf16[1024,256]{1,0:T(8,128)(2,1)S(1)} %get-tuple-element.60.refs_1_.refs_2_.refs_3_), channel_id=1, source_target_pairs={{0,64},{16,80},{32,96},{48,112},{64,0},{80,16},{96,32},{112,48},{1... | collective-permute-start | bytes 1572872 | tf_op jit(solution)/shard_map/ppermute | solution.py:548
  15.9 15.5 %collective-permute-start.5 = (f32[2,1024]{1,0:T(2,128)S(1)}, f32[2,1024]{1,0:T(2,128)S(1)}, u32[]{:S(2)}, u32[]{:S(2)}) collective-permute-start(f32[2,1024]{1,0:T(2,128)S(1)} %copy-done.7), channel_id=1, source_target_pairs={{0,64},{16,80},{32,96},{48,112},{64,0},{80,16},{96,32},{112,48},{1... | collective-permute-start | bytes 24584 | tf_op jit(solution)/shard_map/ppermute | solution.py:548
  24.8 10.3 %collective-permute-start.2 = (bf16[512,256]{1,0:T(8,128)(2,1)S(1)}, bf16[512,256]{1,0:T(8,128)(2,1)S(1)}, u32[]{:S(2)}, u32[]{:S(2)}) collective-permute-start(bf16[512,256]{1,0:T(8,128)(2,1)S(1)} %get-tuple-element.58), channel_id=1, source_target_pairs={{0,16},{16,32},{32,48},{48,0},{64,80},{80,96},{96,112},{112,64},{1... | collective-permute-start | bytes 786440 | tf_op jit(solution)/shard_map/ppermute | solution.py:545
  24.9 10.2 %collective-permute-start.3 = (bf16[512,256]{1,0:T(8,128)(2,1)S(1)}, bf16[512,256]{1,0:T(8,128)(2,1)S(1)}, u32[]{:S(2)}, u32[]{:S(2)}) collective-permute-start(bf16[512,256]{1,0:T(8,128)(2,1)S(1)} %get-tuple-element.59), channel_id=1, source_target_pairs={{0,48},{16,0},{32,16},{48,32},{64,112},{80,64},{96,80},{112,96},{1... | collective-permute-start | bytes 786440 | tf_op jit(solution)/shard_map/ppermute | solution.py:545
  37.6 4.4 %collective-permute-start.6 = (f32[4,1024]{1,0:T(4,128)S(1)}, f32[4,1024]{1,0:T(4,128)S(1)}, u32[]{:S(2)}, u32[]{:S(2)}) collective-permute-start(f32[4,1024]{1,0:T(4,128)S(1)} %get-tuple-element.65.refs_0_), channel_id=1, source_target_pairs={{0,64},{16,80},{32,96},{48,112},{64,0},{80,16},{96,32},{112,48},{1... | collective-permute-start | bytes 49160 | tf_op jit(solution)/shard_map/ppermute | solution.py:548
  48.1 11.5 %collective-permute-start.7 = (bf16[256,1024]{1,0:T(8,128)(2,1)S(1)}, bf16[256,1024]{1,0:T(8,128)(2,1)S(1)}, u32[]{:S(2)}, u32[]{:S(2)}) collective-permute-start(bf16[256,1024]{1,0:T(8,128)(2,1)S(1)} %get-tuple-element.83), channel_id=1, source_target_pairs={{0,64},{16,80},{32,96},{48,112},{64,0},{80,16},{96,32},{112,48},{1... | collective-permute-start | bytes 1572872 | tf_op jit(solution)/shard_map/ppermute | solution.py:548
  53.6 13.7 %collective-permute-start.11 = (bf16[1024,256]{1,0:T(8,128)(2,1)S(1)}, bf16[1024,256]{1,0:T(8,128)(2,1)S(1)}, u32[]{:S(2)}, u32[]{:S(2)}) collective-permute-start(bf16[1024,256]{1,0:T(8,128)(2,1)S(1)} %get-tuple-element.92), channel_id=1, source_target_pairs={{0,16},{16,32},{32,48},{48,0},{64,80},{80,96},{96,112},{112,64},{1... | collective-permute-start | bytes 1572872 | tf_op jit(solution)/shard_map/ppermute | solution.py:545
  53.7 13.6 %collective-permute-start.10 = (bf16[1024,256]{1,0:T(8,128)(2,1)S(1)}, bf16[1024,256]{1,0:T(8,128)(2,1)S(1)}, u32[]{:S(2)}, u32[]{:S(2)}) collective-permute-start(bf16[1024,256]{1,0:T(8,128)(2,1)S(1)} %get-tuple-element.91), channel_id=1, source_target_pairs={{0,48},{16,0},{32,16},{48,32},{64,112},{80,64},{96,80},{112,96},{1... | collective-permute-start | bytes 1572872 | tf_op jit(solution)/shard_map/ppermute | solution.py:545
  56.4 18.0 %collective-permute-start.9 = (bf16[1024,256]{1,0:T(8,128)(2,1)S(1)}, bf16[1024,256]{1,0:T(8,128)(2,1)S(1)}, u32[]{:S(2)}, u32[]{:S(2)}) collective-permute-start(bf16[1024,256]{1,0:T(8,128)(2,1)S(1)} %get-tuple-element.90), channel_id=1, source_target_pairs={{0,32},{16,48},{32,0},{48,16},{64,96},{80,112},{96,64},{112,80},{1... | collective-permute-start | bytes 1572872 | tf_op jit(solution)/shard_map/ppermute | solution.py:545
  59.7 14.7 %copy-start = (bf16[1024,1024]{1,0:T(8,128)(2,1)S(1)}, bf16[1024,1024]{1,0:T(8,128)(2,1)}, u32[]{:S(2)}) copy-start(bf16[1024,1024]{1,0:T(8,128)(2,1)} %refs_0_.5) | copy-start | bytes 6291460
  59.7 14.7 %copy-start.2 = (bf16[1024,512]{1,0:T(8,128)(2,1)S(1)}, bf16[1024,512]{1,0:T(8,128)(2,1)}, u32[]{:S(2)}) copy-start(bf16[1024,512]{1,0:T(8,128)(2,1)} %get-tuple-element.87.refs_2_) | copy-start | bytes 3145732
  59.7 14.7 %copy-start.3 = (f32[1024,256]{1,0:T(8,128)S(1)}, f32[1024,256]{1,0:T(8,128)}, u32[]{:S(2)}) copy-start(f32[1024,256]{1,0:T(8,128)} %get-tuple-element.88.refs_3_) | copy-start | bytes 3145732
  59.7 14.7 %copy-start.5 = (bf16[512,256]{1,0:T(8,128)(2,1)S(1)}, bf16[512,256]{1,0:T(8,128)(2,1)}, u32[]{:S(2)}) copy-start(bf16[512,256]{1,0:T(8,128)(2,1)} %refs_1_.5) | copy-start | bytes 786436
  62.8 22.3 %collective-permute-start.8 = (bf16[2568,128]{1,0:T(8,128)(2,1)S(1)}, bf16[2568,128]{1,0:T(8,128)(2,1)S(1)}, u32[]{:S(2)}, u32[]{:S(2)}) collective-permute-start(bf16[2568,128]{1,0:T(8,128)(2,1)S(1)} %get-tuple-element.86), channel_id=1, source_target_pairs={{0,1},{1,0},{2,3},{3,2},{4,5},{5,4},{6,7},{7,6},{8,9},{9,8},{10,11... | collective-permute-start | bytes 1972232 | tf_op jit(solution)/shard_map/ppermute | solution.py:551
  77.2 7.9 %collective-permute-start.12 = (bf16[2560,128]{1,0:T(8,128)(2,1)S(1)}, bf16[2560,128]{1,0:T(8,128)(2,1)S(1)}, u32[]{:S(2)}, u32[]{:S(2)}) collective-permute-start(bf16[2560,128]{1,0:T(8,128)(2,1)S(1)} %get-tuple-element.94), channel_id=1, source_target_pairs={{0,1},{1,0},{2,3},{3,2},{4,5},{5,4},{6,7},{7,6},{8,9},{9,8},{10,11... | collective-permute-start | bytes 1966088 | tf_op jit(solution)/shard_map/ppermute | solution.py:551
  141.4 5.2 %collective-permute-start.13 = (bf16[64,80,128]{2,1,0:T(8,128)(2,1)S(1)}, bf16[64,80,128]{2,1,0:T(8,128)(2,1)S(1)}, u32[]{:S(2)}, u32[]{:S(2)}) collective-permute-start(bf16[64,80,128]{2,1,0:T(8,128)(2,1)S(1)} %all_to_all.11.refs_0_), channel_id=1, source_target_pairs={{0,1},{1,0},{2,3},{3,2},{4,5},{5,4},{6,7},{7,6},{8,9},{9,8},{10,11... | collective-permute-start | bytes 3932168 | tf_op jit(solution)/shard_map/ppermute | solution.py:551

commit v3 on v2

--- a/solution.py
+++ b/solution.py
@@ -18,6 +18,9 @@
 LANES = 128
 ROWS = 256
 HOPS = (0, 1, NZ - 1, 2)
+ROW = ("x_hi", "z")
+EVERY = (*ROW, "x_lo", "y", "core")
+PEERS = ("x_hi", "x_lo", "y", "z")
 
 
 def dot(a, b, dims=(1, 0)):
@@ -47,13 +50,12 @@
 
 def forward_kernel(feats, first, second, *results):
     def step(k, carry):
-        for r in range(0, 2 * ROWS, ROWS):
-            here = pl.ds(pl.multiple_of(k * 2 * ROWS + r, ROWS), ROWS)
-            for ref, value in zip(results, forward_of(feats[here, :], first[...], second[...])):
-                ref[here, :] = value
+        here = pl.ds(pl.multiple_of(k * ROWS, ROWS), ROWS)
+        for ref, value in zip(results, forward_of(feats[here, :], first[...], second[...])):
+            ref[here, :] = value
         return carry
 
-    lax.fori_loop(0, feats.shape[0] // (2 * ROWS), step, 0)
+    lax.fori_loop(0, feats.shape[0] // ROWS, step, 0)
 
 
 def forward_shapes(m, hid, emb):
@@ -79,9 +81,9 @@
 
 def first_forward_kernel(steps, *refs):
     feats, first, second, sharp, chosen = refs[:5]
-    results_out, meta_out = refs[5:8], refs[8]
-    x, w1, w2, sharp_in, chosen_in, meta = refs[9:15]
-    results, sems, out_sems = refs[15:18], refs[18], refs[19]
+    results_out, meta_out = refs[5:6], refs[6]
+    x, w1, w2, sharp_in, chosen_in, meta = refs[7:13]
+    results, sems, out_sems = refs[13:14], refs[14], refs[15]
     blocks = [pl.ds(k * ROWS, ROWS) for k in range(steps)]
     copy = pltpu.make_async_copy
     feats_in = [copy(feats.at[here], x.at[here], sems.at[k]) for k, here in enumerate(blocks)]
@@ -103,7 +105,7 @@
         feats_in[k].wait()
         here = blocks[k]
         values = forward_of(x[here, :], w1[...], w2[...])
-        for j in range(3):
+        for j in range(len(results)):
             results[j][here, :] = values[j]
             copies.append(copy(results[j].at[here], results_out[j].at[here], out_sems.at[j, k]))
             copies[-1].start()
@@ -113,7 +115,7 @@
             for which, rows in enumerate((sharp_in[...].astype(F32), chosen_in[...].astype(F32))):
                 for i in range(rows.shape[0]):
                     meta[which : which + 1, i * LANES : (i + 1) * LANES] = rows[i : i + 1, :]
-            copies.append(copy(meta, meta_out, out_sems.at[3, 0]))
+            copies.append(copy(meta, meta_out, out_sems.at[1, 0]))
             copies[-1].start()
     for one in copies:
         one.wait()
@@ -122,21 +124,21 @@
 def first_tower_forward(feats, first, second, sharp, chosen):
     m, f = feats.shape
     steps = m // ROWS
-    results = [*forward_shapes(m, *second.shape), ((2, m), F32)]
+    results = [forward_shapes(m, *second.shape)[0], ((2, m), F32)]
     sharp, chosen = sharp.reshape(-1, LANES), chosen.reshape(-1, LANES)
     operands = (feats, first, second, sharp, chosen)
     in_hbm = pl.BlockSpec(memory_space=pltpu.HBM)
     return pl.pallas_call(
         functools.partial(first_forward_kernel, steps),
         in_specs=[in_hbm] * 5,
-        out_specs=[in_hbm] * 4,
+        out_specs=[in_hbm] * 2,
         out_shape=[jax.ShapeDtypeStruct(*s) for s in results],
         scratch_shapes=[
             *[pltpu.VMEM(x.shape, x.dtype) for x in operands],
-            pltpu.VMEM(*results[3]),
-            *[pltpu.VMEM(*s) for s in results[:3]],
+            pltpu.VMEM(*results[1]),
+            pltpu.VMEM(*results[0]),
             pltpu.SemaphoreType.DMA((steps + 5,)),
-            pltpu.SemaphoreType.DMA((4, steps)),
+            pltpu.SemaphoreType.DMA((2, steps)),
         ],
         cost_estimate=forward_cost(m, f, *second.shape),
         compiler_params=grant(58),
@@ -145,9 +147,8 @@
 
 
 def first_item(slot, rows):
-    row = lax.axis_index("row")
-    z = lax.rem(row, NZ)
-    return (row - z + lax.rem(z + (NZ - HOPS[slot]), NZ)) * rows
+    column = lax.rem(lax.axis_index("z") + (NZ - HOPS[slot]), NZ)
+    return (lax.axis_index("x_hi") * NZ + column) * rows
 
 
 def scores_kernel(blocks, n_items, n_users, n_sums, last, *refs):
@@ -494,8 +495,7 @@
 
 def sum_over_all(user_parts, item_parts, loss, shapes, other_core, count):
     (kept_users, sent_users), (kept_items, sent_items) = user_parts, item_parts
-    peers = ("row", "chip")
-    n_peers = lax.axis_size("row") * lax.axis_size("chip")
+    n_peers = math.prod(lax.axis_size(axis) for axis in PEERS)
     share = kept_users.shape[0] // n_peers
     got_users, got_items = other_core(sent_users), other_core(sent_items)
     to_sum = pl.pallas_call(
@@ -506,7 +506,7 @@
         compiler_params=grant(10),
         name="pair",
     )(kept_users, got_users, kept_items, got_items, loss)
-    parts = lax.all_to_all(to_sum, peers, 0, 0, tiled=True)
+    parts = lax.all_to_all(to_sum, PEERS, 0, 0, tiled=True)
     to_share, loss = pl.pallas_call(
         functools.partial(share_kernel, count),
         in_specs=in_vmem(1),
@@ -518,7 +518,7 @@
         compiler_params=grant(10),
         name="share",
     )(parts)
-    mine = lax.all_to_all(to_share, peers, 0, 0, tiled=True)
+    mine = lax.all_to_all(to_share, PEERS, 0, 0, tiled=True)
     theirs = other_core(mine)
     grads = unpack(mine, shapes)
     grads = unpack(theirs, shapes, tuple(grads))
@@ -537,25 +537,28 @@
 ):
     m, f = customer_inputs.shape
     hid, emb = customer_final_weights.shape
-    n_row = lax.axis_size("row")
-    n_all = n_row * lax.axis_size("chip") * lax.axis_size("core")
+    n_row = math.prod(lax.axis_size(axis) for axis in ROW)
+    n_all = math.prod(lax.axis_size(axis) for axis in EVERY)
 
     def along_z(value, hop):
         pairs = [(a * NZ + k, a * NZ + (k + hop) % NZ) for a in range(n_row // NZ) for k in range(NZ)]
-        return lax.ppermute(value, "row", pairs)
+        return lax.ppermute(value, ROW, pairs)
 
     def partner(value):
-        return lax.ppermute(value, "row", [(k, (k + NZ) % n_row) for k in range(n_row)])
+        return lax.ppermute(value, ROW, [(k, (k + NZ) % n_row) for k in range(n_row)])
 
     def other_core(value):
         return lax.ppermute(value, "core", [(0, 1), (1, 0)])
 
-    item_vec, item_hidden, item_out, meta = first_tower_forward(
+    item_vec, meta = first_tower_forward(
         candidate_inputs,
         candidate_initial_weights,
         candidate_final_weights,
         affinity_sharpness,
         correct_candidate_index,
+    )
+    _, item_hidden, item_out = tower_forward(
+        candidate_inputs, candidate_initial_weights, candidate_final_weights
     )
     metas = (meta, partner(meta))
     items = [item_vec]
@@ -622,9 +625,8 @@
 
 def solution(mesh):
     n_row, n_col = mesh.devices.shape
-    fine = Mesh(mesh.devices.reshape(n_row, n_col // 2, 2), ("row", "chip", "core"))
-    every = ("row", "chip", "core")
-    placed = (P(every, None), P(every, None), P(every), P(every), P(), P(), P(), P())
+    fine = Mesh(mesh.devices.reshape(n_row // NZ, NZ, n_col // 8, 4, 2), EVERY)
+    placed = (P(EVERY, None), P(EVERY, None), P(EVERY), P(EVERY), P(), P(), P(), P())
     return jax.shard_map(
         step, mesh=fine, in_specs=placed, out_specs=(P(), P(), P(), P(), P()), check_vma=False
     )

time: 149 us -> 142 us (0.953)
  waiting for transfers between devices: 21.8 us -> 17.5 us
  Pallas kernels: 38.6 us -> 42.6 us
  starting transfers between devices: 32.2 us -> 28.6 us
  blocking collectives: 54.7 us -> 52.3 us
    pallas_call x1 -> x2, Pallas kernels: 2.22 us -> 6.54 us  [tower_forward(): pl.pallas_call(forward_kernel, in_specs=in_vmem(3), out_specs=in_vmem(3),...]
    ppermute x11, waiting for transfers between devices: 19 us -> 14.7 us  [the longest x7 13.4 us: along_z(): return lax.ppermute(value, ROW, pairs)]
    ppermute x3, starting transfers between devices: 13.2 us -> 9.35 us  [other_core(): return lax.ppermute(value, 'core', [(0, 1), (1, 0)])]
    all_to_all x2, blocking collectives: 54.7 us -> 52.3 us  [the longest x1 27.5 us: sum_over_all(): parts = lax.all_to_all(to_sum, PEERS, 0, 0, tiled=True)]
  transfers between devices with their start and end apart: 14 -> 14, of which waited for: 7 -> 6; matrix products, arithmetic and copies ran while one was open for 0% -> 0% of each run, Pallas kernels for 14% -> 18%
where the time goes in v3:
time: 142 us
  blocking collectives  52.3 us (37%)
  Pallas kernels  42.6 us (30%)
  starting transfers between devices  28.6 us (20%)
  waiting for transfers between devices  17.5 us (12%)
    all_to_all x1, blocking collectives, sum_over_all(): parts = lax.all_to_all(to_sum, PEERS, 0, 0, tiled=True)  27.5 us
    all_to_all x1, blocking collectives, sum_over_all(): mine = lax.all_to_all(to_share, PEERS, 0, 0, tiled=True)  24.7 us
    ppermute x7, waiting for transfers between devices, along_z(): return lax.ppermute(value, ROW, pairs)  13.4 us
    ppermute x7, starting transfers between devices, along_z(): return lax.ppermute(value, ROW, pairs)  10.3 us
    pallas_call x5, Pallas kernels, vector_grads(): pl.pallas_call(functools.partial(vectors_kernel, plan, unit), in_specs=in...  10.1 us
    pallas_call x4, Pallas kernels, scores(): pl.pallas_call(functools.partial(scores_kernel, blocks, len(items), len(u...  10 us
    ppermute x3, starting transfers between devices, other_core(): return lax.ppermute(value, 'core', [(0, 1), (1, 0)])  9.35 us
    ppermute x4, starting transfers between devices, partner(): lax.ppermute(value, ROW, [(k, (k + NZ) % n_row) for k in range(n_row)])  8.91 us
  transfers between devices with their start and end apart: 14, of which 6 were waited for; matrix products, arithmetic and copies ran while one was open for 0% of the time, Pallas kernels for 18%

profile of v3, /device:TPU:1, one launch (start us, length us, event | category | flops | bytes accessed | tf_op | source)
XLA Modules:
  0.0 142.0 jit_solution(13880685950658740850)
XLA Ops:
  0.7 5.3 %tower_forward.4 = (bf16[1024,256]{1,0:T(8,128)(2,1)}, f32[2,1024]{1,0:T(2,128)}) custom-call(bf16[1024,1024]{1,0:T(8,128)(2,1)} %refs_0_.5, bf16[1024,512]{1,0:T(8,128)(2,1)} %first.3, bf16[512,256]{1,0:T(8,128)(2,1)} %refs_1_.5, bf16[8,128]{1,0:T(8,128)(2,1)} %bitcast.4, s32[8,128]{1,0:T(8,128)} %bitcast.3), custom_call_target="tpu_custom_call" | custom-call | flops 1342177280 | bytes 4718592 | tf_op jit(solution)/shard_map/tower_forward/pallas_call | solution.py:131
  6.0 2.5 %collective-permute-start = (bf16[1024,256]{1,0:T(8,128)(2,1)}, bf16[1024,256]{1,0:T(8,128)(2,1)S(1)}, u32[]{:S(2)}, u32[]{:S(2)}) collective-permute-start(bf16[1024,256]{1,0:T(8,128)(2,1)} %get-tuple-element.57.refs_0_.refs_2_), channel_id=1, source_target_pairs={{0,16},{16,32},{32,48},{48,0},{64,80},{80,96},{96,112},{112,64},{1... | collective-permute-start | bytes 1572872 | tf_op jit(solution)/shard_map/ppermute | solution.py:545
  8.5 2.2 %collective-permute-start.1 = (bf16[1024,256]{1,0:T(8,128)(2,1)}, bf16[1024,256]{1,0:T(8,128)(2,1)S(1)}, u32[]{:S(2)}, u32[]{:S(2)}) collective-permute-start(bf16[1024,256]{1,0:T(8,128)(2,1)} %get-tuple-element.57.refs_0_.refs_2_), channel_id=1, source_target_pairs={{0,48},{16,0},{32,16},{48,32},{64,112},{80,64},{96,80},{112,96},{1... | collective-permute-start | bytes 1572872 | tf_op jit(solution)/shard_map/ppermute | solution.py:545
  10.7 2.9 %tower_forward.3 = (bf16[1024,256]{1,0:T(8,128)(2,1)S(1)}, bf16[1024,512]{1,0:T(8,128)(2,1)S(1)}, f32[1024,256]{1,0:T(8,128)S(1)}) custom-call(bf16[1024,1024]{1,0:T(8,128)(2,1)S(1)} %copy-done.1, bf16[1024,512]{1,0:T(8,128)(2,1)S(1)} %copy-done.6, bf16[512,256]{1,0:T(8,128)(2,1)S(1)} %copy-done.4), custom_call_target="tpu_custom_call" | custom-call | flops 1342177280 | bytes 4718592 | tf_op jit(solution)/shard_map/tower_forward/pallas_call | solution.py:71
  13.6 2.8 %collective-permute-start.4 = (bf16[1024,256]{1,0:T(8,128)(2,1)S(1)}, bf16[1024,256]{1,0:T(8,128)(2,1)S(1)}, u32[]{:S(2)}, u32[]{:S(2)}) collective-permute-start(bf16[1024,256]{1,0:T(8,128)(2,1)S(1)} %get-tuple-element.60.refs_1_.refs_2_.refs_3_), channel_id=1, source_target_pairs={{0,64},{16,80},{32,96},{48,112},{64,0},{80,16},{96,32},{112,48},{1... | collective-permute-start | bytes 1572872 | tf_op jit(solution)/shard_map/ppermute | solution.py:548
  16.6 5.8 %collective-permute-done.a.refs_0_.refs_1_.refs_3_.refs_2_ = bf16[1024,256]{1,0:T(8,128)(2,1)S(1)} collective-permute-done((bf16[1024,256]{1,0:T(8,128)(2,1)}, bf16[1024,256]{1,0:T(8,128)(2,1)S(1)}, u32[]{:S(2)}, u32[]{:S(2)}) %collective-permute-start) | collective-permute-done | bytes 524320 | tf_op jit(solution)/shard_map/ppermute | solution.py:545
  23.0 2.3 %collective-permute-start.3 = (bf16[512,256]{1,0:T(8,128)(2,1)S(1)}, bf16[512,256]{1,0:T(8,128)(2,1)S(1)}, u32[]{:S(2)}, u32[]{:S(2)}) collective-permute-start(bf16[512,256]{1,0:T(8,128)(2,1)S(1)} %get-tuple-element.59), channel_id=1, source_target_pairs={{0,48},{16,0},{32,16},{48,32},{64,112},{80,64},{96,80},{112,96},{1... | collective-permute-start | bytes 786440 | tf_op jit(solution)/shard_map/ppermute | solution.py:545
  26.6 2.5 %scores.5 = (bf16[1024,1024]{1,0:T(8,128)(2,1)S(1)}, bf16[1024,1024]{1,0:T(8,128)(2,1)S(1)}, f32[2,1024]{1,0:T(2,128)S(1)}) custom-call(bf16[1024,256]{1,0:T(8,128)(2,1)S(1)} %collective-permute-done.a.refs_0_.refs_1_.refs_3_.refs_2_, bf16[1024,256]{1,0:T(8,128)(2,1)S(1)} %collective-permute-done.1.b.refs_1_.refs_2_.refs_4_, ...), custom_call_target="tpu_custom_call" | custom-call | flops 1073741824 | bytes 4194304 | tf_op jit(solution)/shard_map/scores/pallas_call | solution.py:206
  29.1 3.7 %scores.6 = (bf16[1024,1024]{1,0:T(8,128)(2,1)S(1)}, bf16[1024,1024]{1,0:T(8,128)(2,1)S(1)}, bf16[1024,1024]{1,0:T(8,128)(2,1)S(1)}, f32[2,1024]{1,0:T(2,128)S(1)}) custom-call(bf16[1024,256]{1,0:T(8,128)(2,1)S(1)} %copy-done.2, bf16[1024,256]{1,0:T(8,128)(2,1)S(1)} %collective-permute-done.a.refs_0_.refs_1_.refs_3_.refs_2_, ...), custom_call_target="tpu_custom_call" | custom-call | flops 1610612736 | bytes 6291456 | tf_op jit(solution)/shard_map/scores/pallas_call | solution.py:206
  32.8 2.5 %scores.7 = (bf16[1024,1024]{1,0:T(8,128)(2,1)S(1)}, bf16[1024,1024]{1,0:T(8,128)(2,1)S(1)}, f32[4,1024]{1,0:T(4,128)S(1)}, bf16[1024,256]{1,0:T(8,128)(2,1)S(1)}) custom-call(bf16[512,256]{1,0:T(8,128)(2,1)S(1)} %collective-permute-done.2.refs_0_, bf16[512,256]{1,0:T(8,128)(2,1)S(1)} %collective-permute-done.3.refs_1_, ...), custom_call_target="tpu_custom_call" | custom-call | flops 1073741824 | bytes 4194304 | tf_op jit(solution)/shard_map/scores/pallas_call | solution.py:206
  35.3 3.0 %collective-permute-start.6 = (f32[4,1024]{1,0:T(4,128)S(1)}, f32[4,1024]{1,0:T(4,128)S(1)}, u32[]{:S(2)}, u32[]{:S(2)}) collective-permute-start(f32[4,1024]{1,0:T(4,128)S(1)} %get-tuple-element.65.refs_0_), channel_id=1, source_target_pairs={{0,64},{16,80},{32,96},{48,112},{64,0},{80,16},{96,32},{112,48},{1... | collective-permute-start | bytes 49160 | tf_op jit(solution)/shard_map/ppermute | solution.py:548
  39.7 2.5 %vector_grads.5 = (bf16[1024,256]{1,0:T(8,128)(2,1)S(1)}, f32[256,1024]{1,0:T(8,128)S(1)}, f32[256,1024]{1,0:T(8,128)S(1)}) custom-call(f32[4,1024]{1,0:T(4,128)S(1)} %get-tuple-element.65.refs_0_, f32[4,1024]{1,0:T(4,128)S(1)} %collective-permute-done.6.refs_1_, bf16[1024,256]{1,0:T(8,128)(2,1)S(1)} %get-tuple-element.70.refs_2_, ...), custom_call_target="tpu_custom_call" | custom-call | flops 2147483648 | bytes 6815744 | tf_op jit(solution)/shard_map/vector_grads/pallas_call | solution.py:335
  42.2 3.6 %vector_grads.6 = (f32[1024,256]{1,0:T(8,128)S(1)}, f32[1024,256]{1,0:T(8,128)S(1)}, f32[1024,256]{1,0:T(8,128)S(1)}, bf16[256,1024]{1,0:T(8,128)(2,1)S(1)}) custom-call(f32[4,1024]{1,0:T(4,128)S(1)} %get-tuple-element.65.refs_0_, f32[4,1024]{1,0:T(4,128)S(1)} %collective-permute-done.6.refs_1_, bf16[1024,256]{1,0:T(8,128)(2,1)S(1)} %copy-done.2, ...), custom_call_target="tpu_custom_call" | custom-call | flops 3221225472 | bytes 8912896 | tf_op jit(solution)/shard_map/vector_grads/pallas_call | solution.py:335
  45.8 2.8 %collective-permute-start.7 = (bf16[256,1024]{1,0:T(8,128)(2,1)S(1)}, bf16[256,1024]{1,0:T(8,128)(2,1)S(1)}, u32[]{:S(2)}, u32[]{:S(2)}) collective-permute-start(bf16[256,1024]{1,0:T(8,128)(2,1)S(1)} %get-tuple-element.83), channel_id=1, source_target_pairs={{0,64},{16,80},{32,96},{48,112},{64,0},{80,16},{96,32},{112,48},{1... | collective-permute-start | bytes 1572872 | tf_op jit(solution)/shard_map/ppermute | solution.py:548
  54.1 3.7 %tower_forward.5 = (bf16[1024,256]{1,0:T(8,128)(2,1)}, bf16[1024,512]{1,0:T(8,128)(2,1)S(1)}, f32[1024,256]{1,0:T(8,128)S(1)}) custom-call(bf16[1024,1024]{1,0:T(8,128)(2,1)S(1)} %copy-done, bf16[1024,512]{1,0:T(8,128)(2,1)S(1)} %copy-done.7, bf16[512,256]{1,0:T(8,128)(2,1)S(1)} %copy-done.3), custom_call_target="tpu_custom_call" | custom-call | flops 1342177280 | bytes 4718592 | tf_op jit(solution)/shard_map/tower_forward/pallas_call | solution.py:71
  59.1 3.2 %tower_backward.2 = (bf16[2560,128]{1,0:T(8,128)(2,1)S(1)}, bf16[2568,128]{1,0:T(8,128)(2,1)S(1)}) custom-call(bf16[1024,1024]{1,0:T(8,128)(2,1)S(1)} %copy-done.1, bf16[512,256]{1,0:T(8,128)(2,1)S(1)} %copy-done.4, bf16[1024,512]{1,0:T(8,128)(2,1)S(1)} %get-tuple-element.55.refs_2_, f32[1024,256]{1,0:T(8,128)S(1)} %get-tuple-element.56.refs_3_, ...), custom_call_target="tpu_custom_call" | custom-call | flops 1610612736 | bytes 6815744 | tf_op jit(solution)/shard_map/tower_backward/pallas_call | solution.py:409
  62.3 4.6 %collective-permute-start.8 = (bf16[2568,128]{1,0:T(8,128)(2,1)S(1)}, bf16[2568,128]{1,0:T(8,128)(2,1)S(1)}, u32[]{:S(2)}, u32[]{:S(2)}) collective-permute-start(bf16[2568,128]{1,0:T(8,128)(2,1)S(1)} %get-tuple-element.86), channel_id=1, source_target_pairs={{0,1},{1,0},{2,3},{3,2},{4,5},{5,4},{6,7},{7,6},{8,9},{9,8},{10,11... | collective-permute-start | bytes 1972232 | tf_op jit(solution)/shard_map/ppermute | solution.py:551
  66.9 6.1 %collective-permute-done.10.refs_6_ = bf16[1024,256]{1,0:T(8,128)(2,1)S(1)} collective-permute-done((bf16[1024,256]{1,0:T(8,128)(2,1)S(1)}, bf16[1024,256]{1,0:T(8,128)(2,1)S(1)}, u32[]{:S(2)}, u32[]{:S(2)}) %collective-permute-start.10) | collective-permute-done | bytes 524320 | tf_op jit(solution)/shard_map/ppermute | solution.py:545
  74.5 2.8 %tower_backward.3 = (bf16[2560,128]{1,0:T(8,128)(2,1)S(1)}, bf16[2560,128]{1,0:T(8,128)(2,1)S(1)}) custom-call(bf16[1024,1024]{1,0:T(8,128)(2,1)S(1)} %copy-done, bf16[512,256]{1,0:T(8,128)(2,1)S(1)} %copy-done.3, bf16[1024,512]{1,0:T(8,128)(2,1)S(1)} %get-tuple-element.87.refs_2_, f32[1024,256]{1,0:T(8,128)S(1)} %get-tuple-element.88.refs_3_, ...), custom_call_target="tpu_custom_call" | custom-call | flops 1610612736 | bytes 6815744 | tf_op jit(solution)/shard_map/tower_backward/pallas_call | solution.py:409
  78.6 1.7 %collective-permute-done.12.got_items = bf16[2560,128]{1,0:T(8,128)(2,1)S(1)} collective-permute-done((bf16[2560,128]{1,0:T(8,128)(2,1)S(1)}, bf16[2560,128]{1,0:T(8,128)(2,1)S(1)}, u32[]{:S(2)}, u32[]{:S(2)}) %collective-permute-start.12) | collective-permute-done | bytes 655392 | tf_op jit(solution)/shard_map/ppermute | solution.py:551
  81.0 27.5 %all_to_all.10.parts = bf16[64,88,128]{2,1,0:T(8,128)(2,1)S(1)} all-to-all(bf16[64,88,128]{2,1,0:T(8,128)(2,1)S(1)} %pair.1), channel_id=1, replica_groups=mesh['x_hi'=2,'z'=4,'x_lo'=2,'y'=4,'core'=2] {'x_hi','x_lo','y','z'}, dimensions={0} | all-to-all | bytes 2883584 | tf_op jit(solution)/shard_map/all_to_all | solution.py:509
  109.4 24.7 %all_to_all.11.refs_0_ = bf16[64,80,128]{2,1,0:T(8,128)(2,1)S(1)} all-to-all(bf16[64,80,128]{2,1,0:T(8,128)(2,1)S(1)} %get-tuple-element.96), channel_id=1, replica_groups=mesh['x_hi'=2,'z'=4,'x_lo'=2,'y'=4,'core'=2] {'x_hi','x_lo','y','z'}, dimensions={0} | all-to-all | bytes 2621440 | tf_op jit(solution)/shard_map/all_to_all | solution.py:521
  134.2 3.4 %collective-permute-start.13 = (bf16[64,80,128]{2,1,0:T(8,128)(2,1)S(1)}, bf16[64,80,128]{2,1,0:T(8,128)(2,1)S(1)}, u32[]{:S(2)}, u32[]{:S(2)}) collective-permute-start(bf16[64,80,128]{2,1,0:T(8,128)(2,1)S(1)} %all_to_all.11.refs_0_), channel_id=1, source_target_pairs={{0,1},{1,0},{2,3},{3,2},{4,5},{5,4},{6,7},{7,6},{8,9},{9,8},{10,11... | collective-permute-start | bytes 3932168 | tf_op jit(solution)/shard_map/ppermute | solution.py:551
  137.6 1.6 %unpack.2 = (f32[1024,512]{1,0:T(8,128)}, f32[512,256]{1,0:T(8,128)}, f32[1024,512]{1,0:T(8,128)}, f32[512,256]{1,0:T(8,128)}) custom-call(bf16[64,80,128]{2,1,0:T(8,128)(2,1)S(1)} %all_to_all.11.refs_0_), custom_call_target="tpu_custom_call" | custom-call | flops 100000000 | bytes 1966080 | tf_op jit(solution)/shard_map/unpack/pallas_call | solution.py:480
  (41 shorter events, 17.2 us)
Async XLA Ops:
  0.6 10.0 %copy-start.1 = (bf16[1024,1024]{1,0:T(8,128)(2,1)S(1)}, bf16[1024,1024]{1,0:T(8,128)(2,1)}, u32[]{:S(2)}) copy-start(bf16[1024,1024]{1,0:T(8,128)(2,1)} %refs_0_.4) | copy-start | bytes 6291460
  0.6 10.0 %copy-start.4 = (bf16[512,256]{1,0:T(8,128)(2,1)S(1)}, bf16[512,256]{1,0:T(8,128)(2,1)}, u32[]{:S(2)}) copy-start(bf16[512,256]{1,0:T(8,128)(2,1)} %refs_1_.4) | copy-start | bytes 786436
  0.7 10.0 %copy-start.6 = (bf16[1024,512]{1,0:T(8,128)(2,1)S(1)}, bf16[1024,512]{1,0:T(8,128)(2,1)}, u32[]{:S(2)}) copy-start(bf16[1024,512]{1,0:T(8,128)(2,1)} %first.2) | copy-start | bytes 3145732
  5.9 10.5 %copy-start.5 = (f32[2,1024]{1,0:T(2,128)S(1)}, f32[2,1024]{1,0:T(2,128)}, u32[]{:S(2)}) copy-start(f32[2,1024]{1,0:T(2,128)} %get-tuple-element.61.refs_2_.refs_3_.refs_4_.refs_5_) | copy-start | bytes 24580
  5.9 19.3 %copy-start.2 = (bf16[1024,256]{1,0:T(8,128)(2,1)S(1)}, bf16[1024,256]{1,0:T(8,128)(2,1)}, u32[]{:S(2)}) copy-start(bf16[1024,256]{1,0:T(8,128)(2,1)} %get-tuple-element.57.refs_0_.refs_2_) | copy-start | bytes 1572868
  6.0 16.5 %collective-permute-start = (bf16[1024,256]{1,0:T(8,128)(2,1)}, bf16[1024,256]{1,0:T(8,128)(2,1)S(1)}, u32[]{:S(2)}, u32[]{:S(2)}) collective-permute-start(bf16[1024,256]{1,0:T(8,128)(2,1)} %get-tuple-element.57.refs_0_.refs_2_), channel_id=1, source_target_pairs={{0,16},{16,32},{32,48},{48,0},{64,80},{80,96},{96,112},{112,64},{1... | collective-permute-start | bytes 1572872 | tf_op jit(solution)/shard_map/ppermute | solution.py:545
  8.5 14.0 %collective-permute-start.1 = (bf16[1024,256]{1,0:T(8,128)(2,1)}, bf16[1024,256]{1,0:T(8,128)(2,1)S(1)}, u32[]{:S(2)}, u32[]{:S(2)}) collective-permute-start(bf16[1024,256]{1,0:T(8,128)(2,1)} %get-tuple-element.57.refs_0_.refs_2_), channel_id=1, source_target_pairs={{0,48},{16,0},{32,16},{48,32},{64,112},{80,64},{96,80},{112,96},{1... | collective-permute-start | bytes 1572872 | tf_op jit(solution)/shard_map/ppermute | solution.py:545
  13.6 15.6 %collective-permute-start.4 = (bf16[1024,256]{1,0:T(8,128)(2,1)S(1)}, bf16[1024,256]{1,0:T(8,128)(2,1)S(1)}, u32[]{:S(2)}, u32[]{:S(2)}) collective-permute-start(bf16[1024,256]{1,0:T(8,128)(2,1)S(1)} %get-tuple-element.60.refs_1_.refs_2_.refs_3_), channel_id=1, source_target_pairs={{0,64},{16,80},{32,96},{48,112},{64,0},{80,16},{96,32},{112,48},{1... | collective-permute-start | bytes 1572872 | tf_op jit(solution)/shard_map/ppermute | solution.py:548
  16.4 12.7 %collective-permute-start.5 = (f32[2,1024]{1,0:T(2,128)S(1)}, f32[2,1024]{1,0:T(2,128)S(1)}, u32[]{:S(2)}, u32[]{:S(2)}) collective-permute-start(f32[2,1024]{1,0:T(2,128)S(1)} %copy-done.5), channel_id=1, source_target_pairs={{0,64},{16,80},{32,96},{48,112},{64,0},{80,16},{96,32},{112,48},{1... | collective-permute-start | bytes 24584 | tf_op jit(solution)/shard_map/ppermute | solution.py:548
  22.5 10.3 %collective-permute-start.2 = (bf16[512,256]{1,0:T(8,128)(2,1)S(1)}, bf16[512,256]{1,0:T(8,128)(2,1)S(1)}, u32[]{:S(2)}, u32[]{:S(2)}) collective-permute-start(bf16[512,256]{1,0:T(8,128)(2,1)S(1)} %get-tuple-element.58), channel_id=1, source_target_pairs={{0,16},{16,32},{32,48},{48,0},{64,80},{80,96},{96,112},{112,64},{1... | collective-permute-start | bytes 786440 | tf_op jit(solution)/shard_map/ppermute | solution.py:545
  23.0 9.9 %collective-permute-start.3 = (bf16[512,256]{1,0:T(8,128)(2,1)S(1)}, bf16[512,256]{1,0:T(8,128)(2,1)S(1)}, u32[]{:S(2)}, u32[]{:S(2)}) collective-permute-start(bf16[512,256]{1,0:T(8,128)(2,1)S(1)} %get-tuple-element.59), channel_id=1, source_target_pairs={{0,48},{16,0},{32,16},{48,32},{64,112},{80,64},{96,80},{112,96},{1... | collective-permute-start | bytes 786440 | tf_op jit(solution)/shard_map/ppermute | solution.py:545
  35.3 4.4 %collective-permute-start.6 = (f32[4,1024]{1,0:T(4,128)S(1)}, f32[4,1024]{1,0:T(4,128)S(1)}, u32[]{:S(2)}, u32[]{:S(2)}) collective-permute-start(f32[4,1024]{1,0:T(4,128)S(1)} %get-tuple-element.65.refs_0_), channel_id=1, source_target_pairs={{0,64},{16,80},{32,96},{48,112},{64,0},{80,16},{96,32},{112,48},{1... | collective-permute-start | bytes 49160 | tf_op jit(solution)/shard_map/ppermute | solution.py:548
  45.8 13.3 %collective-permute-start.7 = (bf16[256,1024]{1,0:T(8,128)(2,1)S(1)}, bf16[256,1024]{1,0:T(8,128)(2,1)S(1)}, u32[]{:S(2)}, u32[]{:S(2)}) collective-permute-start(bf16[256,1024]{1,0:T(8,128)(2,1)S(1)} %get-tuple-element.83), channel_id=1, source_target_pairs={{0,64},{16,80},{32,96},{48,112},{64,0},{80,16},{96,32},{112,48},{1... | collective-permute-start | bytes 1572872 | tf_op jit(solution)/shard_map/ppermute | solution.py:548
  48.6 18.3 %collective-permute-start.9 = (bf16[1024,256]{1,0:T(8,128)(2,1)S(1)}, bf16[1024,256]{1,0:T(8,128)(2,1)S(1)}, u32[]{:S(2)}, u32[]{:S(2)}) collective-permute-start(bf16[1024,256]{1,0:T(8,128)(2,1)S(1)} %get-tuple-element.90), channel_id=1, source_target_pairs={{0,32},{16,48},{32,0},{48,16},{64,96},{80,112},{96,64},{112,80},{1... | collective-permute-start | bytes 1572872 | tf_op jit(solution)/shard_map/ppermute | solution.py:545
  50.9 22.1 %collective-permute-start.10 = (bf16[1024,256]{1,0:T(8,128)(2,1)S(1)}, bf16[1024,256]{1,0:T(8,128)(2,1)S(1)}, u32[]{:S(2)}, u32[]{:S(2)}) collective-permute-start(bf16[1024,256]{1,0:T(8,128)(2,1)S(1)} %get-tuple-element.91), channel_id=1, source_target_pairs={{0,48},{16,0},{32,16},{48,32},{64,112},{80,64},{96,80},{112,96},{1... | collective-permute-start | bytes 1572872 | tf_op jit(solution)/shard_map/ppermute | solution.py:545
  51.6 2.5 %copy-start = (bf16[1024,1024]{1,0:T(8,128)(2,1)S(1)}, bf16[1024,1024]{1,0:T(8,128)(2,1)}, u32[]{:S(2)}) copy-start(bf16[1024,1024]{1,0:T(8,128)(2,1)} %refs_0_.5) | copy-start | bytes 6291460
  51.6 2.5 %copy-start.3 = (bf16[512,256]{1,0:T(8,128)(2,1)S(1)}, bf16[512,256]{1,0:T(8,128)(2,1)}, u32[]{:S(2)}) copy-start(bf16[512,256]{1,0:T(8,128)(2,1)} %refs_1_.5) | copy-start | bytes 786436
  51.6 2.5 %copy-start.7 = (bf16[1024,512]{1,0:T(8,128)(2,1)S(1)}, bf16[1024,512]{1,0:T(8,128)(2,1)}, u32[]{:S(2)}) copy-start(bf16[1024,512]{1,0:T(8,128)(2,1)} %first.3) | copy-start | bytes 3145732
  52.9 21.5 %collective-permute-start.11 = (bf16[1024,256]{1,0:T(8,128)(2,1)S(1)}, bf16[1024,256]{1,0:T(8,128)(2,1)S(1)}, u32[]{:S(2)}, u32[]{:S(2)}) collective-permute-start(bf16[1024,256]{1,0:T(8,128)(2,1)S(1)} %get-tuple-element.92), channel_id=1, source_target_pairs={{0,16},{16,32},{32,48},{48,0},{64,80},{80,96},{96,112},{112,64},{1... | collective-permute-start | bytes 1572872 | tf_op jit(solution)/shard_map/ppermute | solution.py:545
  62.3 18.0 %collective-permute-start.8 = (bf16[2568,128]{1,0:T(8,128)(2,1)S(1)}, bf16[2568,128]{1,0:T(8,128)(2,1)S(1)}, u32[]{:S(2)}, u32[]{:S(2)}) collective-permute-start(bf16[2568,128]{1,0:T(8,128)(2,1)S(1)} %get-tuple-element.86), channel_id=1, source_target_pairs={{0,1},{1,0},{2,3},{3,2},{4,5},{5,4},{6,7},{7,6},{8,9},{9,8},{10,11... | collective-permute-start | bytes 1972232 | tf_op jit(solution)/shard_map/ppermute | solution.py:551
  77.3 3.0 %collective-permute-start.12 = (bf16[2560,128]{1,0:T(8,128)(2,1)S(1)}, bf16[2560,128]{1,0:T(8,128)(2,1)S(1)}, u32[]{:S(2)}, u32[]{:S(2)}) collective-permute-start(bf16[2560,128]{1,0:T(8,128)(2,1)S(1)} %get-tuple-element.94), channel_id=1, source_target_pairs={{0,1},{1,0},{2,3},{3,2},{4,5},{5,4},{6,7},{7,6},{8,9},{9,8},{10,11... | collective-permute-start | bytes 1966088 | tf_op jit(solution)/shard_map/ppermute | solution.py:551
  134.2 6.1 %collective-permute-start.13 = (bf16[64,80,128]{2,1,0:T(8,128)(2,1)S(1)}, bf16[64,80,128]{2,1,0:T(8,128)(2,1)S(1)}, u32[]{:S(2)}, u32[]{:S(2)}) collective-permute-start(bf16[64,80,128]{2,1,0:T(8,128)(2,1)S(1)} %all_to_all.11.refs_0_), channel_id=1, source_target_pairs={{0,1},{1,0},{2,3},{3,2},{4,5},{5,4},{6,7},{7,6},{8,9},{9,8},{10,11... | collective-permute-start | bytes 3932168 | tf_op jit(solution)/shard_map/ppermute | solution.py:551
